TPU v7x, 32 devices: a whole 2x2x4 slice. The times are simulated.
32 devices in a mesh: tile: 8 (over y, x, core), head: 4 (over z).
Axes of the slice: x: 2, y: 2, z: 4, core: 2. Of those that a mesh axis runs over, the one named last changes fastest.
Arguments:
- latent: bfloat16 [16, 512, 512], P('tile', 'head'), may hold values from -6 to 6
- norm1_gain: float32 [512], replicated, may hold values from 0.25 to 1.75
- norm1_shift: float32 [512], replicated, may hold values from -1.75 to 1.75
- conv1_weight: bfloat16 [3, 3, 512, 512], replicated, may hold values from -0.09375 to 0.09375
- conv1_bias: float32 [512], replicated, may hold values from -1.75 to 1.75
- norm2_gain: float32 [512], replicated, may hold values from 0.25 to 1.75
- norm2_shift: float32 [512], replicated, may hold values from -1.75 to 1.75
- conv2_weight: bfloat16 [3, 3, 512, 512], replicated, may hold values from -0.09375 to 0.09375
- conv2_bias: float32 [512], replicated, may hold values from -1.75 to 1.75
- norm3_gain: float32 [512], replicated, may hold values from 0.25 to 1.75
- norm3_shift: float32 [512], replicated, may hold values from -1.75 to 1.75
- query_weight: bfloat16 [512, 512], replicated, may hold values from -2 to 2
- query_bias: float32 [512], replicated, may hold values from -3 to 3
- key_weight: bfloat16 [512, 512], replicated, may hold values from -2 to 2
- value_weight: bfloat16 [512, 512], replicated, may hold values from -0.25 to 0.25
- value_bias: float32 [512], replicated, may hold values from -3 to 3
- out_weight: bfloat16 [512, 512], replicated, may hold values from -0.5 to 0.5
- out_bias: float32 [512], replicated, may hold values from -1.75 to 1.75
Outputs:
- block_out: bfloat16 [16, 512, 512], P('tile', 'head')
All inputs are finite; a program needn't handle non-finite values.
Results may differ from a plain program's by a relative error of at most 0.01615.
Values may be sent and summed in bfloat16 or wider, within the bound.
A program may use at most 128 MiB of HBM per device.

v0:
```python
import functools

import jax
import jax.numpy as jnp
from jax import lax
from jax.experimental import pallas as pl
from jax.experimental.pallas import tpu as pltpu
from jax.sharding import PartitionSpec as P

C = 512
GROUPS = 32
WIDTH = C // GROUPS
EPS = 1e-06
MESH = pl.DeviceIdType.MESH
VMEM = pl.BlockSpec(memory_space=pltpu.VMEM)


def moved(tile, head, tiles, heads, dt, dh):
    return (lax.rem(tile + dt + tiles, tiles), lax.rem(head + dh + heads, heads))


def greet_all(tile, head, tiles, heads):
    total = tiles * heads
    me = tile * heads + head
    barrier = pltpu.get_barrier_semaphore()

    def greet(k, carry):
        peer = lax.rem(me + k, total)
        pl.semaphore_signal(
            barrier, inc=1, device_id=(peer // heads, lax.rem(peer, heads)), device_id_type=MESH
        )
        return carry

    lax.fori_loop(1, total, greet, 0)


def group_dot(row, onehot, axis):
    return lax.dot_general(
        jnp.broadcast_to(row, (8, row.shape[1])),
        onehot,
        (((1,), (axis,)), ((), ())),
        precision=lax.Precision.HIGHEST,
        preferred_element_type=jnp.float32,
    )[:1]


def membership():
    channel = lax.broadcasted_iota(jnp.int32, (C, 128), 0)
    first = lax.broadcasted_iota(jnp.int32, (C, 128), 1) * WIDTH
    return jnp.where((channel >= first) & (channel < first + WIDTH), 1.0, 0.0)


def store_stats(values, stat_ref):
    onehot = membership()
    values = values.astype(jnp.float32)
    sums = group_dot(jnp.sum(values, axis=0, keepdims=True), onehot, 0)
    mean = sums / (values.shape[0] * WIDTH)
    deviation = values - group_dot(mean, onehot, 1)
    stat_ref[0:1] = mean
    stat_ref[1:2] = group_dot(jnp.sum(deviation * deviation, axis=0, keepdims=True), onehot, 0)


def store_norm(slots_ref, norm_ref, count):
    onehot = membership()
    slots = slots_ref[...]
    total = slots.shape[0]
    sums = jnp.sum(slots, axis=0)
    mean = sums[0:1] / total
    gap = slots[:, 0:1, :] - mean[None]
    variance = (sums[1:2] + count * jnp.sum(gap * gap, axis=0)) / (total * count)
    norm_ref[0:1] = group_dot(mean, onehot, 1)
    norm_ref[1:2] = group_dot(lax.rsqrt(variance + EPS), onehot, 1)


def stats_copy(stat_ref, slots_ref, send, recv, me, total, heads, k):
    peer = lax.rem(me + k, total)
    return pltpu.make_async_remote_copy(
        src_ref=stat_ref,
        dst_ref=slots_ref.at[k],
        send_sem=send.at[k],
        recv_sem=recv.at[k],
        device_id=(peer // heads, lax.rem(peer, heads)),
        device_id_type=MESH,
    )


def exchange_kernel(tiles, heads, plan, npay, *refs):
    values_ref, pays = refs[0], refs[1 : 1 + npay]
    norm_ref, gots = refs[1 + npay], refs[2 + npay : 2 + npay + len(plan)]
    stat_ref, slots_ref, s_send, s_recv, p_send, p_recv = refs[2 + npay + len(plan) :]
    total = tiles * heads
    tile, head = lax.axis_index("tile"), lax.axis_index("head")
    me = tile * heads + head
    greet_all(tile, head, tiles, heads)
    store_stats(values_ref[...], stat_ref)
    slots_ref[0] = stat_ref[...]
    pl.semaphore_wait(pltpu.get_barrier_semaphore(), total - 1)
    copies = []
    for i, (src, dt, dh) in enumerate(plan):
        copies.append(
            pltpu.make_async_remote_copy(
                src_ref=pays[src],
                dst_ref=gots[i],
                send_sem=p_send.at[i],
                recv_sem=p_recv.at[i],
                device_id=moved(tile, head, tiles, heads, dt, dh),
                device_id_type=MESH,
            )
        )
    one = functools.partial(stats_copy, stat_ref, slots_ref, s_send, s_recv, me, total, heads)

    def begin(k, carry):
        one(k).start()
        return carry

    def finish(k, carry):
        one(k).wait()
        return carry

    lax.fori_loop(1, total, begin, 0)
    for copy in copies:
        copy.start()
    lax.fori_loop(1, total, finish, 0)
    store_norm(slots_ref, norm_ref, values_ref.shape[0] * WIDTH)
    for copy in copies:
        copy.wait()


def exchange(cid, stat, payloads, plan):
    tiles, heads = lax.axis_size("tile"), lax.axis_size("head")
    total = tiles * heads
    outs = [jax.ShapeDtypeStruct((2, C), jnp.float32)]
    outs += [jax.ShapeDtypeStruct(payloads[s].shape, payloads[s].dtype) for s, _, _ in plan]
    return pl.pallas_call(
        functools.partial(exchange_kernel, tiles, heads, plan, len(payloads)),
        out_shape=outs,
        in_specs=[VMEM] * (1 + len(payloads)),
        out_specs=[VMEM] * len(outs),
        scratch_shapes=[
            pltpu.VMEM((2, 128), jnp.float32),
            pltpu.VMEM((total, 2, 128), jnp.float32),
            pltpu.SemaphoreType.DMA((total,)),
            pltpu.SemaphoreType.DMA((total,)),
            pltpu.SemaphoreType.DMA((len(plan),)),
            pltpu.SemaphoreType.DMA((len(plan),)),
        ],
        compiler_params=pltpu.CompilerParams(collective_id=cid, has_side_effects=True),
        name="exchange_%d" % cid,
    )(stat, *payloads)


def gather_kernel(
    tiles, heads, res_ref, norm_ref, kv_ref, q_ref, stat_ref, slots_ref, *sems
):
    s_send, s_recv, z_send, z_recv, c_send, c_recv, q_send, q_recv = sems
    total = tiles * heads
    tile, head = lax.axis_index("tile"), lax.axis_index("head")
    me = tile * heads + head
    partner = (tile + 1 - 2 * lax.rem(tile, 2), head)
    greet_all(tile, head, tiles, heads)
    store_stats(res_ref[...], stat_ref)
    slots_ref[0] = stat_ref[...]
    pl.semaphore_wait(pltpu.get_barrier_semaphore(), total - 1)
    one = functools.partial(stats_copy, stat_ref, slots_ref, s_send, s_recv, me, total, heads)

    def begin(k, carry):
        one(k).start()
        return carry

    def finish(k, carry):
        one(k).wait()
        return carry

    lax.fori_loop(1, total, begin, 0)

    def zcopy(k):
        return pltpu.make_async_remote_copy(
            src_ref=res_ref,
            dst_ref=kv_ref.at[0, k],
            send_sem=z_send.at[k],
            recv_sem=z_recv.at[k],
            device_id=(tile, lax.rem(head + k, heads)),
            device_id_type=MESH,
        )

    def ccopy(k):
        return pltpu.make_async_remote_copy(
            src_ref=res_ref if k == 0 else kv_ref.at[0, k],
            dst_ref=kv_ref.at[1, k],
            send_sem=c_send.at[k],
            recv_sem=c_recv.at[k],
            device_id=partner,
            device_id_type=MESH,
        )

    def qcopy(j):
        return pltpu.make_async_remote_copy(
            src_ref=res_ref,
            dst_ref=q_ref.at[j],
            send_sem=q_send.at[j],
            recv_sem=q_recv.at[j],
            device_id=(lax.rem(tile + 2 * j, tiles), head),
            device_id_type=MESH,
        )

    for k in range(1, heads):
        zcopy(k).start()
    for j in range(1, tiles // 2):
        qcopy(j).start()
    ccopy(0).start()
    kv_ref[0, 0] = res_ref[...]
    q_ref[0] = res_ref[...]
    lax.fori_loop(1, total, finish, 0)
    store_norm(slots_ref, norm_ref, res_ref.shape[0] * WIDTH)
    for k in range(1, heads):
        zcopy(k).wait_recv()
        ccopy(k).start()
    for k in range(1, heads):
        zcopy(k).wait_send()
    for j in range(1, tiles // 2):
        qcopy(j).wait()
    for k in range(heads):
        ccopy(k).wait()


def gather(cid, resid):
    tiles, heads = lax.axis_size("tile"), lax.axis_size("head")
    total = tiles * heads
    n, c = resid.shape
    dma = pltpu.SemaphoreType.DMA
    return pl.pallas_call(
        functools.partial(gather_kernel, tiles, heads),
        out_shape=[
            jax.ShapeDtypeStruct((2, C), jnp.float32),
            jax.ShapeDtypeStruct((2, heads, n, c), resid.dtype),
            jax.ShapeDtypeStruct((tiles // 2, n, c), resid.dtype),
        ],
        in_specs=[VMEM],
        out_specs=[VMEM] * 3,
        scratch_shapes=[
            pltpu.VMEM((2, 128), jnp.float32),
            pltpu.VMEM((total, 2, 128), jnp.float32),
        ]
        + [dma((total,))] * 2
        + [dma((heads,))] * 4
        + [dma((tiles // 2,))] * 2,

        compiler_params=pltpu.CompilerParams(collective_id=cid, has_side_effects=True),
        name="gather_%d" % cid,
    )(resid)


def attend_kernel(
    tiles,
    heads,
    q_ref,
    k_ref,
    v_ref,
    res_ref,
    w_ref,
    b_ref,
    out_ref,
    o_scr,
    og_scr,
    l_scr,
    lg_scr,
    o_send,
    o_recv,
    l_send,
    l_recv,
):
    tile, head = lax.axis_index("tile"), lax.axis_index("head")
    half = tiles // 2
    n = res_ref.shape[0]
    barrier = pltpu.get_barrier_semaphore()
    for j in range(1, half):
        pl.semaphore_signal(
            barrier,
            inc=1,
            device_id=(lax.rem(tile + 2 * j, tiles), head),
            device_id_type=MESH,
        )
    pl.semaphore_wait(barrier, half - 1)
    softmax_scale = 1.0 / C**0.5

    def copies(j):
        owner = (lax.rem(tile + tiles - 2 * j, tiles), head)
        return [
            pltpu.make_async_remote_copy(
                src_ref=src.at[j],
                dst_ref=dst.at[j],
                send_sem=send.at[j],
                recv_sem=recv.at[j],
                device_id=owner,
                device_id_type=MESH,
            )
            for src, dst, send, recv in (
                (o_scr, og_scr, o_send, o_recv),
                (l_scr, lg_scr, l_send, l_recv),
            )
        ]

    def compute(j, o_to, l_to):
        scores = jnp.dot(q_ref[j], k_ref[...], preferred_element_type=jnp.float32) * softmax_scale
        peak = jnp.max(scores, axis=1, keepdims=True)
        expo = jnp.exp(scores - peak)
        total = jnp.sum(expo, axis=1, keepdims=True)
        weighted = jnp.dot(expo.astype(jnp.bfloat16), v_ref[...], preferred_element_type=jnp.float32)
        lse = jnp.broadcast_to(peak + jnp.log(total), (n, 128))
        l_to[j] = jnp.transpose(lse)[:8]
        o_to[j] = (weighted / total).astype(jnp.bfloat16)

    def step(j, carry):
        compute(j, o_scr, l_scr)
        for copy in copies(j):
            copy.start()
        return carry

    lax.fori_loop(1, half, step, 0)
    compute(0, og_scr, lg_scr)
    for j in range(1, half):
        for copy in copies(j):
            copy.wait()
    peak = lg_scr[0]
    for j in range(1, half):
        peak = jnp.maximum(peak, lg_scr[j])
    weights = [jnp.exp(lg_scr[j] - peak) for j in range(half)]
    total = weights[0]
    for j in range(1, half):
        total = total + weights[j]
    mixed = jnp.zeros((n, C), jnp.float32)
    for j in range(half):
        column = jnp.transpose(jnp.broadcast_to((weights[j] / total)[:1], (128, n)))[:, :1]
        mixed = mixed + column * og_scr[j].astype(jnp.float32)
    out = jnp.dot(mixed.astype(jnp.bfloat16), w_ref[...], preferred_element_type=jnp.float32)
    out_ref[...] = (res_ref[...].astype(jnp.float32) + out + b_ref[...]).astype(jnp.bfloat16)


def attend(cid, queries, keys, values, resid, weight, bias):
    tiles, heads = lax.axis_size("tile"), lax.axis_size("head")
    half = tiles // 2
    n = resid.shape[0]
    dma = pltpu.SemaphoreType.DMA((half,))
    return pl.pallas_call(
        functools.partial(attend_kernel, tiles, heads),
        out_shape=jax.ShapeDtypeStruct(resid.shape, resid.dtype),
        in_specs=[VMEM] * 6,
        out_specs=VMEM,
        scratch_shapes=[pltpu.VMEM((half, n, C), jnp.bfloat16)] * 2
        + [pltpu.VMEM((half, 8, n), jnp.float32)] * 2
        + [dma] * 4,
        compiler_params=pltpu.CompilerParams(collective_id=cid, has_side_effects=True),
        name="attend_%d" % cid,
    )(queries, keys, values, resid, weight, bias)


def conv_kernel(act_ref, w_ref, b_ref, out_ref, lhs):
    rows, cols = act_ref.shape[0] - 2, act_ref.shape[1] - 2

    @pl.when(pl.program_id(0) == 0)
    def unfold():
        for dj in range(3):
            moved_cols = act_ref[:, dj : dj + cols, :]
            for di in range(3):
                tap = 3 * di + dj
                lhs[:, tap * C : (tap + 1) * C] = moved_cols[di : di + rows].reshape(rows * cols, C)

    out_ref[...] = (
        jnp.dot(lhs[...], w_ref[...], preferred_element_type=jnp.float32) + b_ref[...]
    )


def conv(act, weight, bias):
    rows, cols = act.shape[0] - 2, act.shape[1] - 2
    part = C // 2
    out = pl.pallas_call(
        conv_kernel,
        grid=(C // part,),
        out_shape=jax.ShapeDtypeStruct((rows * cols, C), jnp.float32),
        in_specs=[
            pl.BlockSpec(act.shape, lambda i: (0, 0, 0)),
            pl.BlockSpec((9 * C, part), lambda i: (0, i)),
            pl.BlockSpec((1, part), lambda i: (0, i)),
        ],
        out_specs=pl.BlockSpec((rows * cols, part), lambda i: (0, i)),
        scratch_shapes=[pltpu.VMEM((rows * cols, 9 * C), jnp.bfloat16)],
        cost_estimate=pl.CostEstimate(
            flops=2 * rows * cols * 9 * C * C, bytes_accessed=18 * C * C, transcendentals=0
        ),
        name="conv_%d" % rows,
    )(act, weight.reshape(9 * C, C), bias.reshape(1, C))
    return out.reshape(rows, cols, C)


def combined(norm, gain, shift):
    return norm[0], norm[1] * gain, shift


def normalize(values, norm):
    mean, scale, shift = norm
    return (values - mean) * scale + shift


def inside(rows, cols, first_row, first_col, all_rows, all_cols):
    r = first_row + lax.broadcasted_iota(jnp.int32, (rows, cols, 1), 0)
    c = first_col + lax.broadcasted_iota(jnp.int32, (rows, cols, 1), 1)
    return (r >= 0) & (r < all_rows) & (c >= 0) & (c < all_cols)


def per_device(
    latent,
    norm1_gain,
    norm1_shift,
    conv1_weight,
    conv1_bias,
    norm2_gain,
    norm2_shift,
    conv2_weight,
    conv2_bias,
    norm3_gain,
    norm3_shift,
    query_weight,
    query_bias,
    key_weight,
    value_weight,
    value_bias,
    out_weight,
    out_bias,
):
    rows, cols, channels = latent.shape
    tiles, heads = lax.axis_size("tile"), lax.axis_size("head")
    tile, head = lax.axis_index("tile"), lax.axis_index("head")
    n = rows * cols
    latent32 = latent.astype(jnp.float32)

    top, bottom = latent[:2], latent[rows - 2 :]
    west, east = latent[:, 0], latent[:, cols - 1]
    payloads = [top, bottom, west, east, west[:2], east[:2], west[rows - 2 :], east[rows - 2 :]]
    plan = (
        (1, 1, 0),
        (0, -1, 0),
        (3, 0, 1),
        (2, 0, -1),
        (7, 1, 1),
        (6, 1, -1),
        (5, -1, 1),
        (4, -1, -1),
    )
    slots, above, below, left, right, al, ar, bl, br = exchange(
        1, latent.reshape(n, C), payloads, plan
    )
    lefts = jnp.concatenate([al, left, bl], axis=0)[:, None]
    rights = jnp.concatenate([ar, right, br], axis=0)[:, None]
    middle = jnp.concatenate([above, latent, below], axis=0)
    wide = jnp.concatenate([lefts, middle, rights], axis=1).astype(jnp.float32)
    first_row, first_col = tile * rows, head * cols
    all_rows, all_cols = rows * tiles, cols * heads
    act1 = jax.nn.silu(normalize(wide, combined(slots, norm1_gain, norm1_shift)))
    mask1 = inside(rows + 4, cols + 2, first_row - 2, first_col - 1, all_rows, all_cols)
    act1 = jnp.where(mask1, act1, 0.0).astype(jnp.bfloat16)
    hidden = conv(act1, conv1_weight, conv1_bias)

    slots, left, right = exchange(
        2,
        hidden[1 : rows + 1].reshape(n, C),
        [hidden[:, 0], hidden[:, cols - 1]],
        ((1, 0, 1), (0, 0, -1)),
    )
    wide = jnp.concatenate([left[:, None], hidden, right[:, None]], axis=1)
    act2 = jax.nn.silu(normalize(wide, combined(slots, norm2_gain, norm2_shift)))
    mask2 = inside(rows + 2, cols + 2, first_row - 1, first_col - 1, all_rows, all_cols)
    act2 = jnp.where(mask2, act2, 0.0).astype(jnp.bfloat16)
    resid = (latent32 + conv(act2, conv2_weight, conv2_bias)).astype(jnp.bfloat16)
    resid = resid.reshape(n, C)

    slots, kv_res, q_res = gather(3, resid)
    norm3 = combined(slots, norm3_gain, norm3_shift)
    kv_in = normalize(kv_res.reshape(-1, C).astype(jnp.float32), norm3).astype(jnp.bfloat16)
    q_in = normalize(q_res.reshape(-1, C).astype(jnp.float32), norm3).astype(jnp.bfloat16)
    queries = (jnp.dot(q_in, query_weight, preferred_element_type=jnp.float32) + query_bias).astype(
        jnp.bfloat16
    )
    keys = lax.dot_general(
        key_weight, kv_in, (((0,), (1,)), ((), ())), preferred_element_type=jnp.float32
    ).astype(jnp.bfloat16)
    values = (
        jnp.dot(kv_in, value_weight, preferred_element_type=jnp.float32) + value_bias
    ).astype(jnp.bfloat16)
    mixed = attend(
        4, queries.reshape(-1, n, C), keys, values, resid, out_weight, out_bias.reshape(1, C)
    )
    return mixed.reshape(rows, cols, C)


def solution(mesh):
    return jax.shard_map(
        per_device,
        mesh=mesh,
        in_specs=(P("tile", "head", None),) + (P(),) * 17,
        out_specs=P("tile", "head", None),
        check_vma=False,
    )
```

profile of v0, /device:TPU:8, one launch (start us, length us, event | category | flops | bytes accessed | tf_op | source)
XLA Modules:
  0.0 120.0 jit_solution(18160799596518748196)
XLA Ops:
  0.2 0.7 fusion.16
  1.5 14.6 %exchange_1.1 = (f32[2,512]{1,0:T(2,128)}, bf16[2,128,512]{2,1,0:T(8,128)(2,1)}, bf16[2,128,512]{2,1,0:T(8,128)(2,1)}, bf16[2,512]{1,0:T(2,128)(2,1)}, bf16[2,51...) custom-call(bf16[256,512]{1,0:T(8,128)(2,1)} %bitcast.43, ...), custom_call_target="tpu_custom_call" | custom-call | tf_op jit(solution)/shard_map/exchange_1/pallas_call | solution.py:134
  16.2 0.7 maximum_bitcast_fusion
  16.9 0.8 fusion.19
  18.3 0.7 maximum_bitcast_fusion.1
  19.0 2.8 %select_convert_fusion.act_ref = bf16[6,130,512]{2,1,0:T(8,128)(2,1)} fusion(bf16[6,1,512]{2,1,0:T(2,128)(2,1)S(1)} %copy.25, bf16[2,128,512]{2,1,0:T(8,128)(2,1)} %get-tuple-element.24, bf16[2,128,512]{2,1,0:T(8,128)(2,1)} %refs_2_.1, bf16[2,128,512]{2,1,0:T(8,128)(2,1)} %get-tuple-element.23, bf16[6,1,512]{2,1,0:T(2,128)(2,1)S(1)} %copy.24, f32[512]{0:T(512)} %param.20, ...), kind=kLoop, calls=%fused_computation.12 | loop fusion | flops 7587840 | bytes 1604364 | tf_op jit(solution)/shard_map/convert_element_type | solution.py:460
  21.9 5.9 %conv_4.1 = f32[512,512]{1,0:T(8,128)} custom-call(bf16[6,130,512]{2,1,0:T(8,128)(2,1)} %select_convert_fusion.act_ref, bf16[4608,512]{1,0:T(8,128)(2,1)} %bitcast.63, f32[1,512]{1,0:T(1,128)} %bitcast.65), custom_call_target="tpu_custom_call" | custom-call | flops 2415919104 | bytes 4718592 | tf_op jit(solution)/shard_map/conv_4/pallas_call | solution.py:376
  27.8 1.0 fusion.15
  30.0 1.9 %slice.45.refs_0_ = f32[256,512]{1,0:T(8,128)} slice(f32[512,512]{1,0:T(8,128)} %conv_4.1), slice={[128:384], [0:512]} | slice | bytes 1048576 | tf_op jit(solution)/shard_map/slice | solution.py:465
  31.9 10.7 %exchange_2.1 = (f32[2,512]{1,0:T(2,128)}, f32[4,512]{1,0:T(4,128)}, f32[4,512]{1,0:T(4,128)}) custom-call(f32[256,512]{1,0:T(8,128)} %slice.45.refs_0_, f32[4,512]{1,0:T(4,128)} %bitcast.53, f32[4,512]{1,0:T(4,128)} %bitcast.52), custom_call_target="tpu_custom_call" | custom-call | tf_op jit(solution)/shard_map/exchange_2/pallas_call | solution.py:134
  42.6 0.7 broadcast_in_dim.51
  43.3 0.8 fusion.18
  44.0 0.7 broadcast_in_dim.52
  44.8 1.3 %select_convert_fusion.1.act_ref = bf16[4,130,512]{2,1,0:T(8,128)(2,1)} fusion(f32[4,1,512]{2,1,0:T(1,128)S(1)} %broadcast_in_dim.52, f32[4,128,512]{2,1,0:T(8,128)S(1)} %bitcast.46, f32[4,1,512]{2,1,0:T(1,128)S(1)} %broadcast_in_dim.51, f32[512]{0:T(512)S(1)} %copy-done.3, f32[512]{0:T(512)S(1)} %mul.61, f32[512]{0:T(512)S(1)} %bitcast.55, ...), kind=kLoop, calls=%fused_computation.16 | loop fusion | flops 2928640 | bytes 1604104 | tf_op jit(solution)/shard_map/convert_element_type | solution.py:472
  46.0 4.4 %conv_2.1 = f32[256,512]{1,0:T(8,128)} custom-call(bf16[4,130,512]{2,1,0:T(8,128)(2,1)} %select_convert_fusion.1.act_ref, bf16[4608,512]{1,0:T(8,128)(2,1)} %bitcast.44, f32[1,512]{1,0:T(1,128)} %bitcast.61), custom_call_target="tpu_custom_call" | custom-call | flops 1207959552 | bytes 4718592 | tf_op jit(solution)/shard_map/conv_2/pallas_call | solution.py:376
  50.4 1.8 %add_convert_fusion.2 = bf16[2,128,512]{2,1,0:T(8,128)(2,1)} fusion(f32[2,128,512]{2,1,0:T(8,128)} %bitcast.49, bf16[2,128,512]{2,1,0:T(8,128)(2,1)S(1)} %copy-done.1), kind=kLoop, calls=%fused_computation.20 | loop fusion | flops 393216 | bytes 1048576 | tf_op jit(solution)/shard_map/convert_element_type | solution.py:473
  52.2 32.7 %gather_3.1 = (f32[2,512]{1,0:T(2,128)}, bf16[2,4,256,512]{3,2,1,0:T(8,128)(2,1)}, bf16[4,256,512]{2,1,0:T(8,128)(2,1)}) custom-call(bf16[256,512]{1,0:T(8,128)(2,1)} %bitcast.47), custom_call_target="tpu_custom_call" | custom-call | tf_op jit(solution)/shard_map/gather_3/pallas_call | solution.py:231
  84.9 0.8 fusion.17
  85.8 2.4 %fusion.2 = bf16[2048,512]{1,0:T(8,128)(2,1)S(1)} fusion(bf16[2,4,256,512]{3,2,1,0:T(8,128)(2,1)} %get-tuple-element.34, f32[512]{0:T(512)S(1)} %copy-done.4, f32[512]{0:T(512)S(1)} %mul.65, f32[512]{0:T(512)S(1)} %bitcast.56), kind=kLoop, calls=%fused_computation.3 | loop fusion | flops 5242880 | bytes 4200448 | tf_op jit(solution)/shard_map/convert_element_type | solution.py:478
  88.2 1.7 %add_convert_fusion.1 = bf16[1024,512]{1,0:T(8,128)(2,1)} fusion(bf16[512,512]{1,0:T(8,128)(2,1)S(1)} %copy-done.8, bf16[1024,512]{1,0:T(8,128)(2,1)S(1)} %bitcast.64, f32[512]{0:T(512)S(1)} %copy-done.10, f32[512]{0:T(512)S(1)} %copy-done.4, f32[512]{0:T(512)S(1)} %mul.65, f32[512]{0:T(512)S(1)} %bitcast.57), kind=kOutput, calls=%fused_computation.11 | convolution fusion | flops 540540928 | bytes 2629632 | tf_op jit(solution)/shard_map/dot_general | solution.py:480
  89.9 2.6 %add_convert_fusion.v_ref = bf16[2048,512]{1,0:T(8,128)(2,1)} fusion(bf16[2048,512]{1,0:T(8,128)(2,1)S(1)} %fusion.2, bf16[512,512]{1,0:T(8,128)(2,1)S(1)} %copy-done, f32[512]{0:T(512)S(1)} %copy-done.11), kind=kOutput, calls=%fused_computation.4 | convolution fusion | flops 1075838976 | bytes 4720640 | tf_op jit(solution)/shard_map/dot_general | solution.py:487
  92.5 2.7 %fusion.3.k_ref = bf16[512,2048]{1,0:T(8,128)(2,1)} fusion(bf16[2048,512]{1,0:T(8,128)(2,1)S(1)} %fusion.2, bf16[512,512]{1,0:T(8,128)(2,1)S(1)} %copy-done.9), kind=kOutput, calls=%fused_computation.6 | convolution fusion | flops 1074790400 | bytes 4718592 | tf_op jit(solution)/shard_map/dot_general | solution.py:483
  95.1 23.2 %attend_4.1 = bf16[256,512]{1,0:T(8,128)(2,1)} custom-call(bf16[4,256,512]{2,1,0:T(8,128)(2,1)} %bitcast.51, bf16[512,2048]{1,0:T(8,128)(2,1)} %fusion.3.k_ref, bf16[2048,512]{1,0:T(8,128)(2,1)} %add_convert_fusion.v_ref, bf16[256,512]{1,0:T(8,128)(2,1)} %bitcast.48, bf16[512,512]{1,0:T(8,128)(2,1)} %w_ref.1, f32[1,512]{1,0:T(1,128)} %bitcast.62), custom_call_target="tpu_custom_call" | custom-call | tf_op jit(solution)/shard_map/attend_4/pallas_call | solution.py:344
  118.3 1.7 %copy.39 = bf16[2,128,512]{2,1,0:T(8,128)(2,1)} copy(bf16[2,128,512]{2,1,0:T(8,128)(2,1)} %bitcast.50) | data formatting | bytes 524288
  (37 shorter events, 2.7 us)
Async XLA Ops:
  0.0 89.9 %copy-start = (bf16[512,512]{1,0:T(8,128)(2,1)S(1)}, bf16[512,512]{1,0:T(8,128)(2,1)}, u32[]{:S(2)}) copy-start(bf16[512,512]{1,0:T(8,128)(2,1)} %param.32) | copy-start | bytes 1572868
  27.8 16.2 %copy-start.5 = (f32[512]{0:T(512)S(1)}, f32[512]{0:T(512)}, u32[]{:S(2)}) copy-start(f32[512]{0:T(512)} %param.23) | copy-start | bytes 6148
  27.8 16.9 %copy-start.2 = (f32[512,512]{1,0:T(8,128)S(1)}, f32[512,512]{1,0:T(8,128)}, u32[]{:S(2)}) copy-start(f32[512,512]{1,0:T(8,128)} %conv_4.1) | copy-start | bytes 3145732
  27.8 16.9 %copy-start.3 = (f32[512]{0:T(512)S(1)}, f32[512]{0:T(512)}, u32[]{:S(2)}) copy-start(f32[512]{0:T(512)} %param.24) | copy-start | bytes 6148
  46.0 4.4 %copy-start.1 = (bf16[2,128,512]{2,1,0:T(8,128)(2,1)S(1)}, bf16[2,128,512]{2,1,0:T(8,128)(2,1)}, u32[]{:S(2)}) copy-start(bf16[2,128,512]{2,1,0:T(8,128)(2,1)} %refs_2_.1) | copy-start | bytes 786436
  46.0 39.7 %copy-start.6 = (f32[512]{0:T(512)S(1)}, f32[512]{0:T(512)}, u32[]{:S(2)}) copy-start(f32[512]{0:T(512)} %param.27) | copy-start | bytes 6148
  46.0 39.7 %copy-start.4 = (f32[512]{0:T(512)S(1)}, f32[512]{0:T(512)}, u32[]{:S(2)}) copy-start(f32[512]{0:T(512)} %param.28) | copy-start | bytes 6148
  85.7 2.4 %copy-start.7 = (bf16[4,256,512]{2,1,0:T(8,128)(2,1)S(1)}, bf16[4,256,512]{2,1,0:T(8,128)(2,1)}, u32[]{:S(2)}) copy-start(bf16[4,256,512]{2,1,0:T(8,128)(2,1)} %get-tuple-element.32) | copy-start | bytes 3145732
  85.7 2.4 %copy-start.8 = (bf16[512,512]{1,0:T(8,128)(2,1)S(1)}, bf16[512,512]{1,0:T(8,128)(2,1)}, u32[]{:S(2)}) copy-start(bf16[512,512]{1,0:T(8,128)(2,1)} %param.29) | copy-start | bytes 1572868
  85.8 2.4 %copy-start.10 = (f32[512]{0:T(512)S(1)}, f32[512]{0:T(512)}, u32[]{:S(2)}) copy-start(f32[512]{0:T(512)} %param.30) | copy-start | bytes 6148
  88.2 1.7 %copy-start.11 = (f32[512]{0:T(512)S(1)}, f32[512]{0:T(512)}, u32[]{:S(2)}) copy-start(f32[512]{0:T(512)} %param.33) | copy-start | bytes 6148
  89.9 2.6 %copy-start.9 = (bf16[512,512]{1,0:T(8,128)(2,1)S(1)}, bf16[512,512]{1,0:T(8,128)(2,1)}, u32[]{:S(2)}) copy-start(bf16[512,512]{1,0:T(8,128)(2,1)} %param.31) | copy-start | bytes 1572868
where the time goes:
time: 121 us; the launch traced here: 120 us
  Pallas kernels  91.5 us (76%)
  local copies, waits for them, and re-layouts  10.8 us (9%)
  other arithmetic  10.5 us (9%)
  matrix products  6.95 us (6%)
    pallas_call x1, Pallas kernels, gather(): pl.pallas_call(functools.partial(gather_kernel, tiles, heads), out_shape=...  32.7 us
    pallas_call x2, Pallas kernels, exchange(): pl.pallas_call(functools.partial(exchange_kernel, tiles, heads, plan, len...  25.3 us
    pallas_call x1, Pallas kernels, attend(): pl.pallas_call(functools.partial(attend_kernel, tiles, heads), out_shape=...  23.2 us
    pallas_call x2, Pallas kernels, conv(): pl.pallas_call(conv_kernel, grid=(C // part,), out_shape=jax.ShapeDtypeSt...  10.3 us
    unnamed x27, local copies, waits for them, and re-layouts  2.92 us
    convert_element_type x1, other arithmetic, per_device(): act1 = jnp.where(mask1, act1, 0.0).astype(jnp.bfloat16)  2.83 us
    dot_general x1, matrix products, per_device(): lax.dot_general(key_weight, kv_in, (((0,), (1,)), ((), ())), preferred_el...  2.66 us
    dot_general x1, matrix products, per_device(): jnp.dot(kv_in, value_weight, preferred_element_type=jnp.float32)  2.59 us

commit v1 on v0

v1 whole, which is shorter than its diff:
```python
import functools
import math

import jax
import jax.numpy as jnp
from jax import lax
from jax.experimental import pallas as pl
from jax.experimental.pallas import tpu as pltpu
from jax.sharding import PartitionSpec as P

C = 512
GROUPS = 32
WIDTH = C // GROUPS
EPS = 1e-06
LANES = 128
PARTS = C // LANES
SHARE = WIDTH // PARTS
PAD = 8
LOG2E = math.log2(math.e)
MESH = pl.DeviceIdType.MESH
VMEM = pl.BlockSpec(memory_space=pltpu.VMEM)
ANY = pl.BlockSpec(memory_space=pl.ANY)


def nt_dot(a, b):
    return lax.dot_general(a, b, (((1,), (1,)), ((), ())), preferred_element_type=jnp.float32)


def nn_dot(a, b):
    return jnp.dot(a, b, preferred_element_type=jnp.float32)


def lane_index(rows):
    return lax.broadcasted_iota(jnp.int32, (rows, LANES), 1)


def group_sum(values):
    lane = lane_index(values.shape[0])
    step = 1
    while step < WIDTH:
        below = pltpu.roll(values, step, 1)
        above = pltpu.roll(values, LANES - step, 1)
        values = values + jnp.where(lane % (2 * step) >= step, below, above)
        step *= 2
    return values


def fold(row):
    return jnp.concatenate([row[:, i * LANES : (i + 1) * LANES] for i in range(PARTS)], axis=0)


def unfold(rows):
    return jnp.concatenate([rows[i : i + 1] for i in range(PARTS)], axis=1)


def local_stats(values):
    count = values.shape[0]
    mean = jnp.sum(values, axis=0, keepdims=True) / count
    deviation = values - mean
    square = jnp.sum(deviation * deviation, axis=0, keepdims=True)
    mean, square = fold(mean), fold(square)
    group_mean = group_sum(mean) / WIDTH
    gap = mean - group_mean
    square = group_sum(square + count * gap * gap)
    lane = lane_index(1)
    packed = jnp.zeros((1, LANES), jnp.float32)
    for i in range(PARTS):
        one = jnp.where(lane % 2 == 0, group_mean[i : i + 1], square[i : i + 1])
        packed = jnp.where((lane % WIDTH) // SHARE == i, one, packed)
    return packed


def merged_stats(slots, count):
    total = slots.shape[0]
    sums = jnp.sum(slots, axis=0)
    mean = sums / total
    gap = slots - mean[None]
    spread = jnp.sum(gap * gap, axis=0)
    variance = (sums + count * pltpu.roll(spread, 1, 1)) / (total * count)
    lane = lane_index(1)
    both = jnp.where(lane % 2 == 0, mean, lax.rsqrt(variance + EPS))
    row = lax.broadcasted_iota(jnp.int32, (2 * PARTS, LANES), 0)
    want = (row % PARTS) * SHARE + row // PARTS
    wide = jnp.where(lane_index(2 * PARTS) % WIDTH == want, both, 0.0)
    wide = group_sum(wide)
    return unfold(wide[:PARTS]), unfold(wide[PARTS:])


def silu(values):
    return values / (1.0 + jnp.exp(-values))


def block_kernel(
    tiles,
    heads,
    lat_ref,
    n1g,
    n1s,
    c1b,
    n2g,
    n2s,
    c2b,
    n3g,
    n3s,
    qb,
    vb,
    ob,
    w1_hbm,
    w2_hbm,
    wq_hbm,
    wk_hbm,
    wv_hbm,
    wo_hbm,
    out_ref,
    w1,
    w2,
    wp,
    act,
    shifted,
    hid,
    row_in,
    row_out,
    col_in,
    col_out,
    corner_in,
    stat_out,
    stat_in,
    norm,
    res,
    kv,
    kn,
    qn,
    qp,
    acc,
    top,
    low,
    o_out,
    o_in,
    l_out,
    l_in,
    w_sem,
    s_send,
    s_recv,
    h_send,
    h_recv,
    z_send,
    z_recv,
    c_send,
    c_recv,
    q_send,
    q_recv,
    o_send,
    o_recv,
    l_send,
    l_recv,
):
    rows, cols, _ = lat_ref.shape
    n = rows * cols
    total = tiles * heads
    half = tiles // 2
    tile, head = lax.axis_index("tile"), lax.axis_index("head")
    me = tile * heads + head
    partner = (tile + 1 - 2 * lax.rem(tile, 2), head)

    weights = [
        pltpu.make_async_copy(src, dst, w_sem.at[i])
        for i, (src, dst) in enumerate(
            (
                (w1_hbm, w1),
                (w2_hbm, w2),
                (wq_hbm, wp.at[0]),
                (wk_hbm, wp.at[1]),
                (wv_hbm, wp.at[2]),
                (wo_hbm, wp.at[3]),
            )
        )
    ]
    for copy in weights:
        copy.start()

    barrier = pltpu.get_barrier_semaphore()

    def greet(k, carry):
        peer = lax.rem(me + k, total)
        pl.semaphore_signal(
            barrier, inc=1, device_id=(peer // heads, lax.rem(peer, heads)), device_id_type=MESH
        )
        return carry

    lax.fori_loop(1, total, greet, 0)

    def remote(src, dst, send, recv, device):
        return pltpu.make_async_remote_copy(
            src_ref=src,
            dst_ref=dst,
            send_sem=send,
            recv_sem=recv,
            device_id=device,
            device_id_type=MESH,
        )

    def stat_copy(phase, k):
        peer = lax.rem(me + k, total)
        return remote(
            stat_out.at[phase],
            stat_in.at[phase, k],
            s_send.at[phase, k],
            s_recv.at[phase, k],
            (peer // heads, lax.rem(peer, heads)),
        )

    def stats_start(phase):
        def begin(k, carry):
            stat_copy(phase, k).start()
            return carry

        lax.fori_loop(1, total, begin, 0)

    def stats_finish(phase, gain, shift):
        def finish(k, carry):
            stat_copy(phase, k).wait()
            return carry

        lax.fori_loop(1, total, finish, 0)
        mean, inverse = merged_stats(stat_in[phase], n * WIDTH)
        norm[0:1] = mean
        norm[1:2] = inverse * gain[...]
        norm[2:3] = shift[...]

    def put_stats(phase, values):
        packed = local_stats(values)
        stat_out[phase] = packed
        stat_in[phase, 0] = packed

    def normalize(values):
        return (values - norm[0:1]) * norm[1:2] + norm[2:3]

    def halo_plan(phase, first_row, last_row):
        first, last = col_out.at[phase, 0], col_out.at[phase, 1]
        plan = [
            (first_row, row_in.at[phase, 1], -1, 0),
            (last_row, row_in.at[phase, 0], 1, 0),
            (first, col_in.at[phase, 1], 0, -1),
            (last, col_in.at[phase, 0], 0, 1),
            (first.at[0], corner_in.at[phase, 3], -1, -1),
            (last.at[0], corner_in.at[phase, 2], -1, 1),
            (first.at[rows - 1], corner_in.at[phase, 1], 1, -1),
            (last.at[rows - 1], corner_in.at[phase, 0], 1, 1),
        ]
        return plan

    def there(dt, dh):
        inside = None
        for place, delta, size in ((tile, dt, tiles), (head, dh, heads)):
            if delta:
                one = place + delta < size if delta > 0 else place + delta >= 0
                inside = one if inside is None else jnp.logical_and(inside, one)
        return inside

    def halo_copy(phase, i, src, dst, dt, dh):
        return remote(
            src, dst, h_send.at[phase, i], h_recv.at[phase, i], (tile + dt, head + dh)
        )

    def halo_start(phase, plan):
        for i, (src, dst, dt, dh) in enumerate(plan):

            @pl.when(there(dt, dh))
            def _(i=i, src=src, dst=dst, dt=dt, dh=dh):
                halo_copy(phase, i, src, dst, dt, dh).start()

    def halo_finish(phase, plan):
        for i, (src, dst, dt, dh) in enumerate(plan):

            @pl.when(there(dt, dh))
            def _(i=i, src=src, dst=dst, dt=dt, dh=dh):
                halo_copy(phase, i, src, dst, dt, dh).wait_send()

            @pl.when(there(-dt, -dh))
            def _(i=i, src=src, dst=dst, dt=dt, dh=dh):
                halo_copy(phase, i, src, dst, dt, dh).wait_recv()

    def put_columns(phase, values):
        for r in range(rows):
            col_out[phase, 0, r] = values[r, 0:1]
            col_out[phase, 1, r] = values[r, cols - 1 : cols]

    def activate(phase, values):
        left, right = head > 0, head < heads - 1
        up, down = tile > 0, tile < tiles - 1

        def active(x):
            return silu(normalize(x))

        for r in range(rows):
            act[1 + r, PAD : PAD + cols] = active(values(r))
            for side, at, inside in ((0, PAD - 1, left), (1, PAD + cols, right)):
                one = active(col_in[phase, side, r])
                act[1 + r, at : at + 1] = jnp.where(inside, one, 0.0)
        for side, at, inside in ((0, 0, up), (1, rows + 1, down)):
            one = active(row_in[phase, side].astype(jnp.float32))
            act[at, PAD : PAD + cols] = jnp.where(inside, one, 0.0)
            for k, place, beside in ((0, PAD - 1, left), (1, PAD + cols, right)):
                one = active(corner_in[phase, 2 * side + k])
                both = jnp.logical_and(inside, beside)
                act[at, place : place + 1] = jnp.where(both, one, 0.0)
        for dj in range(3):
            start = PAD - 1 + dj
            for r in range(rows + 2):
                shifted[dj, r] = act[r, start : start + cols].astype(jnp.bfloat16)

    def conv(weight):
        result = None
        for di in range(3):
            for dj in range(3):
                tap = 3 * di + dj
                lhs = shifted[dj, di : di + rows].reshape(n, C)
                one = nn_dot(lhs, weight[tap * C : (tap + 1) * C])
                result = one if result is None else result + one
        return result

    put_columns(0, lat_ref[...].astype(jnp.float32))
    put_stats(0, lat_ref[...].astype(jnp.float32).reshape(n, C))
    pl.semaphore_wait(barrier, total - 1)
    plan = halo_plan(0, lat_ref.at[0], lat_ref.at[rows - 1])
    stats_start(0)
    halo_start(0, plan)
    halo_finish(0, plan)
    stats_finish(0, n1g, n1s)
    activate(0, lambda r: lat_ref[r].astype(jnp.float32))
    weights[0].wait()
    hid[...] = (conv(w1) + c1b[...]).reshape(rows, cols, C)

    put_stats(1, hid[...].reshape(n, C))
    put_columns(1, hid[...])
    row_out[0] = hid[0].astype(jnp.bfloat16)
    row_out[1] = hid[rows - 1].astype(jnp.bfloat16)
    plan = halo_plan(1, row_out.at[0], row_out.at[1])
    stats_start(1)
    halo_start(1, plan)
    halo_finish(1, plan)
    stats_finish(1, n2g, n2s)
    activate(1, lambda r: hid[r])
    weights[1].wait()
    res[...] = (
        lat_ref[...].astype(jnp.float32).reshape(n, C) + (conv(w2) + c2b[...])
    ).astype(jnp.bfloat16)

    put_stats(2, res[...].astype(jnp.float32))
    stats_start(2)

    def z_copy(k):
        return remote(
            res,
            kv.at[0, k],
            z_send.at[k],
            z_recv.at[k],
            (tile, lax.rem(head + k, heads)),
        )

    def c_copy(k, src):
        return remote(src, kv.at[1, k], c_send.at[k], c_recv.at[k], partner)

    def q_copy(j):
        return remote(
            res, qn.at[j], q_send.at[j], q_recv.at[j], (lax.rem(tile + 2 * j, tiles), head)
        )

    c_copy(0, res).start()
    for k in range(1, heads):
        z_copy(k).start()

    def q_begin(j, carry):
        q_copy(j).start()
        return carry

    lax.fori_loop(1, half, q_begin, 0)
    stats_finish(2, n3g, n3s)
    for copy in weights[2:]:
        copy.wait()

    def normed(values):
        return normalize(values.astype(jnp.float32)).astype(jnp.bfloat16)

    scale = LOG2E / C**0.5

    def make_query(j, source):
        query = (nn_dot(normed(source), wp[0]) + qb[...]).astype(jnp.bfloat16)
        qp[j] = (nt_dot(query, wp[1]) * scale).astype(jnp.bfloat16)
        top[j] = jnp.full((n, LANES), -jnp.inf, jnp.float32)
        low[j] = jnp.zeros((n, LANES), jnp.float32)
        acc[j] = jnp.zeros((n, C), jnp.float32)

    make_query(0, res[...])

    def attend(j):
        scores = nt_dot(qp[j], kn[...])
        before = top[j][:, :1]
        peak = jnp.maximum(before, jnp.max(scores, axis=1, keepdims=True))
        expo = jnp.exp2(scores - peak).astype(jnp.bfloat16)
        fade = jnp.exp2(before - peak)
        sums = low[j][:, :1] * fade + jnp.sum(expo.astype(jnp.float32), axis=1, keepdims=True)
        top[j] = jnp.broadcast_to(peak, (n, LANES))
        low[j] = jnp.broadcast_to(sums, (n, LANES))
        acc[j] = acc[j] * fade + nn_dot(expo, kn[...])

    c_copy(0, res).wait()
    kn[0:n] = normed(res[...])
    kn[n : 2 * n] = normed(kv[1, 0])
    attend(0)

    def q_finish(j, carry):
        q_copy(j).wait()
        make_query(j, qn[j])
        attend(j)
        return carry

    lax.fori_loop(1, half, q_finish, 0)

    def column(k, carry):
        z_copy(k).wait()
        c_copy(k, kv.at[0, k]).start()
        kn[0:n] = normed(kv[0, k])
        c_copy(k, kv.at[0, k]).wait()
        kn[n : 2 * n] = normed(kv[1, k])

        def one(j, inner):
            attend(j)
            return inner

        lax.fori_loop(0, half, one, 0)
        return carry

    lax.fori_loop(1, heads, column, 0)

    def give_copies(j):
        owner = (lax.rem(tile + tiles - 2 * j, tiles), head)
        return [
            remote(o_out.at[j], o_in.at[j], o_send.at[j], o_recv.at[j], owner),
            remote(l_out.at[j], l_in.at[j], l_send.at[j], l_recv.at[j], owner),
        ]

    def finish(j, o_to, l_to):
        level = top[j] + jnp.log2(low[j])
        l_to[j] = jnp.transpose(level)[:8]
        o_to[j] = (acc[j] / low[j][:, :1]).astype(jnp.bfloat16)

    def give(j, carry):
        finish(j, o_out, l_out)
        for copy in give_copies(j):
            copy.start()
        return carry

    lax.fori_loop(1, half, give, 0)
    finish(0, o_in, l_in)

    def take(j, carry):
        for copy in give_copies(j):
            copy.wait()
        return carry

    lax.fori_loop(1, half, take, 0)
    peak = l_in[0]
    for j in range(1, half):
        peak = jnp.maximum(peak, l_in[j])
    shares = [jnp.exp2(l_in[j] - peak) for j in range(half)]
    whole = shares[0]
    for j in range(1, half):
        whole = whole + shares[j]
    mixed = jnp.zeros((n, C), jnp.float32)
    for j in range(half):
        share = jnp.transpose(jnp.broadcast_to((shares[j] / whole)[:1], (LANES, n)))[:, :1]
        mixed = mixed + share * o_in[j].astype(jnp.float32)
    attended = (nn_dot(mixed.astype(jnp.bfloat16), wp[2]) + vb[...]).astype(jnp.bfloat16)
    out = nn_dot(attended, wp[3]) + ob[...]
    out_ref[...] = (res[...].astype(jnp.float32) + out).astype(jnp.bfloat16)


def per_device(
    latent,
    norm1_gain,
    norm1_shift,
    conv1_weight,
    conv1_bias,
    norm2_gain,
    norm2_shift,
    conv2_weight,
    conv2_bias,
    norm3_gain,
    norm3_shift,
    query_weight,
    query_bias,
    key_weight,
    value_weight,
    value_bias,
    out_weight,
    out_bias,
):
    rows, cols, _ = latent.shape
    tiles, heads = lax.axis_size("tile"), lax.axis_size("head")
    n = rows * cols
    total = tiles * heads
    half = tiles // 2
    vectors = [
        v.reshape(1, C)
        for v in (
            norm1_gain,
            norm1_shift,
            conv1_bias,
            norm2_gain,
            norm2_shift,
            conv2_bias,
            norm3_gain,
            norm3_shift,
            query_bias,
            value_bias,
            out_bias,
        )
    ]
    matrices = [
        conv1_weight.reshape(9 * C, C),
        conv2_weight.reshape(9 * C, C),
        query_weight,
        key_weight,
        value_weight,
        out_weight,
    ]
    bf16, f32 = jnp.bfloat16, jnp.float32
    dma = pltpu.SemaphoreType.DMA
    out = pl.pallas_call(
        functools.partial(block_kernel, tiles, heads),
        out_shape=jax.ShapeDtypeStruct((n, C), bf16),
        in_specs=[VMEM] * (1 + len(vectors)) + [ANY] * len(matrices),
        out_specs=VMEM,
        scratch_shapes=[
            pltpu.VMEM((9 * C, C), bf16),
            pltpu.VMEM((9 * C, C), bf16),
            pltpu.VMEM((4, C, C), bf16),
            pltpu.VMEM((rows + 2, cols + 2 * PAD, C), f32),
            pltpu.VMEM((3, rows + 2, cols, C), bf16),
            pltpu.VMEM((rows, cols, C), f32),
            pltpu.VMEM((2, 2, cols, C), bf16),
            pltpu.VMEM((2, cols, C), bf16),
            pltpu.VMEM((2, 2, rows, 1, C), f32),
            pltpu.VMEM((2, 2, rows, 1, C), f32),
            pltpu.VMEM((2, 4, 1, C), f32),
            pltpu.VMEM((3, 1, LANES), f32),
            pltpu.VMEM((3, total, 1, LANES), f32),
            pltpu.VMEM((8, C), f32),
            pltpu.VMEM((n, C), bf16),
            pltpu.VMEM((2, heads, n, C), bf16),
            pltpu.VMEM((2 * n, C), bf16),
            pltpu.VMEM((half, n, C), bf16),
            pltpu.VMEM((half, n, C), bf16),
            pltpu.VMEM((half, n, C), f32),
            pltpu.VMEM((half, n, LANES), f32),
            pltpu.VMEM((half, n, LANES), f32),
            pltpu.VMEM((half, n, C), bf16),
            pltpu.VMEM((half, n, C), bf16),
            pltpu.VMEM((half, 8, n), f32),
            pltpu.VMEM((half, 8, n), f32),
            dma((6,)),
            dma((3, total)),
            dma((3, total)),
            dma((2, 8)),
            dma((2, 8)),
            dma((heads,)),
            dma((heads,)),
            dma((heads,)),
            dma((heads,)),
            dma((half,)),
            dma((half,)),
            dma((half,)),
            dma((half,)),
            dma((half,)),
            dma((half,)),
        ],
        compiler_params=pltpu.CompilerParams(collective_id=1, has_side_effects=True),
        name="middle_block",
    )(latent, *vectors, *matrices)
    return out.reshape(rows, cols, C)


def solution(mesh):
    return jax.shard_map(
        per_device,
        mesh=mesh,
        in_specs=(P("tile", "head", None),) + (P(),) * 17,
        out_specs=P("tile", "head", None),
        check_vma=False,
    )
```

time: 121 us -> 76.3 us (0.63)
  the two profiles are of different devices: /device:TPU:8 before, /device:TPU:0 now
where the time goes in v1:
time: 76.3 us; the launch traced here: 76.1 us
  Pallas kernels  74.4 us (98%)
  local copies, waits for them, and re-layouts  1.67 us (2%)
    pallas_call x1, Pallas kernels, per_device(): pl.pallas_call(functools.partial(block_kernel, tiles, heads), out_shape=j...  74.4 us
    unnamed x1, local copies, waits for them, and re-layouts  1.67 us

profile of v1, /device:TPU:0, one launch (start us, length us, event | category | flops | bytes accessed | tf_op | source)
XLA Modules:
  0.0 76.1 jit_solution(1044350106380465524)
XLA Ops:
  0.0 74.4 %middle_block.1 = bf16[256,512]{1,0:T(8,128)(2,1)} custom-call(bf16[2,128,512]{2,1,0:T(8,128)(2,1)} %lat_ref.1, f32[1,512]{1,0:T(1,128)} %bitcast.17, f32[1,512]{1,0:T(1,128)} %bitcast.18, f32[1,512]{1,0:T(1,128)} %bitcast.19, f32[1,512]{1,0:T(1,128)} %bitcast.20, f32[1,512]{1,0:T(1,128)} %bitcast.21, f32[1,512]{1,0:T(1,128)} %bitcast.22, ...), custom_call_target="tpu_custom_call" | custom-call | tf_op jit(solution)/shard_map/middle_block/pallas_call | solution.py:530
  74.4 1.7 %copy.20 = bf16[2,128,512]{2,1,0:T(8,128)(2,1)} copy(bf16[2,128,512]{2,1,0:T(8,128)(2,1)} %bitcast.16) | data formatting | bytes 524288

commit v2 on v1

--- a/solution.py
+++ b/solution.py
@@ -19,7 +19,11 @@
 LOG2E = math.log2(math.e)
 MESH = pl.DeviceIdType.MESH
 VMEM = pl.BlockSpec(memory_space=pltpu.VMEM)
-ANY = pl.BlockSpec(memory_space=pl.ANY)
+HBM = pl.BlockSpec(memory_space=pltpu.HBM)
+VECTORS = 11
+CHUNKS = 2
+DIRECT = 2
+VMEM_LIMIT = 56 * 1024 * 1024
 
 
 def nt_dot(a, b):
@@ -93,90 +97,67 @@
 def block_kernel(
     tiles,
     heads,
-    lat_ref,
-    n1g,
-    n1s,
-    c1b,
-    n2g,
-    n2s,
-    c2b,
-    n3g,
-    n3s,
-    qb,
-    vb,
-    ob,
-    w1_hbm,
-    w2_hbm,
-    wq_hbm,
-    wk_hbm,
-    wv_hbm,
-    wo_hbm,
-    out_ref,
-    w1,
-    w2,
-    wp,
-    act,
-    shifted,
-    hid,
-    row_in,
-    row_out,
-    col_in,
-    col_out,
-    corner_in,
-    stat_out,
-    stat_in,
-    norm,
-    res,
-    kv,
-    kn,
-    qn,
-    qp,
-    acc,
-    top,
-    low,
-    o_out,
-    o_in,
-    l_out,
-    l_in,
-    w_sem,
-    s_send,
-    s_recv,
-    h_send,
-    h_recv,
-    z_send,
-    z_recv,
-    c_send,
-    c_recv,
-    q_send,
-    q_recv,
-    o_send,
-    o_recv,
-    l_send,
-    l_recv,
+    lat_hbm,
+    *refs,
 ):
+    vec_hbm, mat_hbm, refs = refs[:VECTORS], refs[VECTORS : VECTORS + 6], refs[VECTORS + 6 :]
+    (
+        out_ref,
+        lat_ref,
+        vec,
+        w1,
+        w2,
+        wp,
+        act,
+        shifted,
+        hid,
+        row_in,
+        row_out,
+        col_in,
+        col_out,
+        corner_in,
+        stat_out,
+        stat_in,
+        norm,
+        res,
+        kv,
+        kn,
+        kt,
+        qn,
+        qp,
+        acc,
+        top,
+        low,
+        o_out,
+        o_in,
+        l_out,
+        l_in,
+        lat_sem,
+        v_sem,
+        w_sem,
+        s_send,
+        s_recv,
+        h_send,
+        h_recv,
+        z_send,
+        z_recv,
+        c_send,
+        c_recv,
+        q_send,
+        q_recv,
+        o_send,
+        o_recv,
+        l_send,
+        l_recv,
+    ) = refs
     rows, cols, _ = lat_ref.shape
     n = rows * cols
     total = tiles * heads
     half = tiles // 2
+    pairs = half // 2
     tile, head = lax.axis_index("tile"), lax.axis_index("head")
     me = tile * heads + head
     partner = (tile + 1 - 2 * lax.rem(tile, 2), head)
-
-    weights = [
-        pltpu.make_async_copy(src, dst, w_sem.at[i])
-        for i, (src, dst) in enumerate(
-            (
-                (w1_hbm, w1),
-                (w2_hbm, w2),
-                (wq_hbm, wp.at[0]),
-                (wk_hbm, wp.at[1]),
-                (wv_hbm, wp.at[2]),
-                (wo_hbm, wp.at[3]),
-            )
-        )
-    ]
-    for copy in weights:
-        copy.start()
 
     barrier = pltpu.get_barrier_semaphore()
 
@@ -187,7 +168,20 @@
         )
         return carry
 
+    latent_copy = pltpu.make_async_copy(lat_hbm, lat_ref, lat_sem)
+    latent_copy.start()
     lax.fori_loop(1, total, greet, 0)
+    vectors = [
+        pltpu.make_async_copy(src, vec.at[i], v_sem.at[i]) for i, src in enumerate(vec_hbm)
+    ]
+    targets = [w1, w2] + [wp.at[i] for i in range(4)]
+    weights = [
+        pltpu.make_async_copy(src, dst, w_sem.at[i])
+        for i, (src, dst) in enumerate(zip(mat_hbm, targets))
+    ]
+    for copy in vectors + weights:
+        copy.start()
+    n1g, n1s, c1b, n2g, n2s, c2b, n3g, n3s, qb, vb, ob = [vec.at[i] for i in range(VECTORS)]
 
     def remote(src, dst, send, recv, device):
         return pltpu.make_async_remote_copy(
@@ -204,8 +198,8 @@
         return remote(
             stat_out.at[phase],
             stat_in.at[phase, k],
-            s_send.at[phase, k],
-            s_recv.at[phase, k],
+            s_send.at[phase],
+            s_recv.at[phase],
             (peer // heads, lax.rem(peer, heads)),
         )
 
@@ -217,11 +211,9 @@
         lax.fori_loop(1, total, begin, 0)
 
     def stats_finish(phase, gain, shift):
-        def finish(k, carry):
-            stat_copy(phase, k).wait()
-            return carry
-
-        lax.fori_loop(1, total, finish, 0)
+        others = stat_in.at[phase, pl.ds(1, total - 1)]
+        for sem in (s_send, s_recv):
+            pltpu.make_async_copy(others, others, sem.at[phase]).wait()
         mean, inverse = merged_stats(stat_in[phase], n * WIDTH)
         norm[0:1] = mean
         norm[1:2] = inverse * gain[...]
@@ -319,119 +311,251 @@
                 result = one if result is None else result + one
         return result
 
-    put_columns(0, lat_ref[...].astype(jnp.float32))
-    put_stats(0, lat_ref[...].astype(jnp.float32).reshape(n, C))
-    pl.semaphore_wait(barrier, total - 1)
-    plan = halo_plan(0, lat_ref.at[0], lat_ref.at[rows - 1])
-    stats_start(0)
-    halo_start(0, plan)
-    halo_finish(0, plan)
-    stats_finish(0, n1g, n1s)
-    activate(0, lambda r: lat_ref[r].astype(jnp.float32))
-    weights[0].wait()
-    hid[...] = (conv(w1) + c1b[...]).reshape(rows, cols, C)
-
-    put_stats(1, hid[...].reshape(n, C))
-    put_columns(1, hid[...])
-    row_out[0] = hid[0].astype(jnp.bfloat16)
-    row_out[1] = hid[rows - 1].astype(jnp.bfloat16)
-    plan = halo_plan(1, row_out.at[0], row_out.at[1])
-    stats_start(1)
-    halo_start(1, plan)
-    halo_finish(1, plan)
-    stats_finish(1, n2g, n2s)
-    activate(1, lambda r: hid[r])
-    weights[1].wait()
-    res[...] = (
-        lat_ref[...].astype(jnp.float32).reshape(n, C) + (conv(w2) + c2b[...])
-    ).astype(jnp.bfloat16)
-
-    put_stats(2, res[...].astype(jnp.float32))
-    stats_start(2)
-
-    def z_copy(k):
+    with jax.named_scope("stats0"):
+        latent_copy.wait()
+        put_columns(0, lat_ref[...].astype(jnp.float32))
+        put_stats(0, lat_ref[...].astype(jnp.float32).reshape(n, C))
+    with jax.named_scope("barrier"):
+        pl.semaphore_wait(barrier, total - 1)
+    with jax.named_scope("send0"):
+        plan = halo_plan(0, lat_ref.at[0], lat_ref.at[rows - 1])
+        stats_start(0)
+        halo_start(0, plan)
+    with jax.named_scope("halo0"):
+        halo_finish(0, plan)
+    with jax.named_scope("norm0"):
+        for copy in vectors:
+            copy.wait()
+        stats_finish(0, n1g, n1s)
+    with jax.named_scope("act0"):
+        activate(0, lambda r: lat_ref[r].astype(jnp.float32))
+    with jax.named_scope("w0"):
+        weights[0].wait()
+    with jax.named_scope("conv0"):
+        hid[...] = (conv(w1) + c1b[...]).reshape(rows, cols, C)
+
+    with jax.named_scope("stats1"):
+        put_stats(1, hid[...].reshape(n, C))
+        put_columns(1, hid[...])
+        row_out[0] = hid[0].astype(jnp.bfloat16)
+        row_out[1] = hid[rows - 1].astype(jnp.bfloat16)
+    with jax.named_scope("send1"):
+        plan = halo_plan(1, row_out.at[0], row_out.at[1])
+        stats_start(1)
+        halo_start(1, plan)
+    with jax.named_scope("halo1"):
+        halo_finish(1, plan)
+    with jax.named_scope("norm1"):
+        stats_finish(1, n2g, n2s)
+    with jax.named_scope("act1"):
+        activate(1, lambda r: hid[r])
+    with jax.named_scope("conv1"):
+        weights[1].wait()
+        res[...] = (
+            lat_ref[...].astype(jnp.float32).reshape(n, C) + (conv(w2) + c2b[...])
+        ).astype(jnp.bfloat16)
+
+    with jax.named_scope("stats2"):
+        put_stats(2, res[...].astype(jnp.float32))
+        stats_start(2)
+
+    def piece(ref, ch):
+        return ref.at[pl.ds(ch * (n // CHUNKS), n // CHUNKS)]
+
+    def z_copy(source, src, way, distance, ch):
         return remote(
-            res,
-            kv.at[0, k],
-            z_send.at[k],
-            z_recv.at[k],
-            (tile, lax.rem(head + k, heads)),
-        )
-
-    def c_copy(k, src):
-        return remote(src, kv.at[1, k], c_send.at[k], c_recv.at[k], partner)
+            piece(src, ch),
+            piece(kv.at[0, source], ch),
+            z_send.at[way, distance, ch],
+            z_recv.at[source, ch],
+            (tile, head + (1 if way else -1) * (distance if distance <= DIRECT else 1)),
+        )
+
+    def reachable(way, distance):
+        return head + distance < heads if way else head - distance >= 0
+
+    def straight(fn):
+        at_end = jnp.logical_or(head == 0, head == heads - 1)
+        farther = tuple(range(2, min(DIRECT, heads - 1) + 1))
+        for distances, chosen in ((farther, at_end), ((1,), True), (farther, ~at_end)):
+            for distance in distances:
+                for ch in range(CHUNKS):
+                    for way in (0, 1):
+
+                        @pl.when(jnp.logical_and(reachable(way, distance), chosen))
+                        def _(way=way, distance=distance, ch=ch):
+                            fn(z_copy(head, res, way, distance, ch))
+
+    def onward(distance, fn, chunks=tuple(range(CHUNKS))):
+        for ch in chunks:
+            for way in (0, 1):
+
+                @pl.when(jnp.logical_and(reachable(1 - way, distance), reachable(way, 1)))
+                def _(way=way, ch=ch):
+                    source = head + (-distance if way else distance)
+                    fn(z_copy(source, kv.at[0, source], way, distance + 1, ch))
+
+    def z_arrived(source, distance, way):
+        def wait():
+            for ch in range(CHUNKS):
+                z_copy(source, res, way, 1, ch).wait_recv()
+
+        if heads - 1 > DIRECT:
+            passed = jnp.logical_and(distance >= DIRECT, reachable(1 - way, 1))
+            pl.when(jnp.logical_not(passed))(wait)
+        else:
+            wait()
+
+    def c_copy(source, src):
+        return remote(
+            src, kv.at[1, source], c_send.at[source], c_recv.at[source], partner
+        )
 
     def q_copy(j):
         return remote(
             res, qn.at[j], q_send.at[j], q_recv.at[j], (lax.rem(tile + 2 * j, tiles), head)
         )
 
-    c_copy(0, res).start()
-    for k in range(1, heads):
-        z_copy(k).start()
-
     def q_begin(j, carry):
         q_copy(j).start()
         return carry
 
-    lax.fori_loop(1, half, q_begin, 0)
-    stats_finish(2, n3g, n3s)
-    for copy in weights[2:]:
-        copy.wait()
+    c_copy(head, res).start()
+    with jax.named_scope("norm2"):
+        straight(lambda copy: copy.start())
+        lax.fori_loop(1, half, q_begin, 0)
+        stats_finish(2, n3g, n3s)
+        for copy in weights[2:]:
+            copy.wait()
 
     def normed(values):
         return normalize(values.astype(jnp.float32)).astype(jnp.bfloat16)
 
     scale = LOG2E / C**0.5
 
-    def make_query(j, source):
+    def make_query(pair, at, source):
         query = (nn_dot(normed(source), wp[0]) + qb[...]).astype(jnp.bfloat16)
-        qp[j] = (nt_dot(query, wp[1]) * scale).astype(jnp.bfloat16)
-        top[j] = jnp.full((n, LANES), -jnp.inf, jnp.float32)
-        low[j] = jnp.zeros((n, LANES), jnp.float32)
-        acc[j] = jnp.zeros((n, C), jnp.float32)
-
-    make_query(0, res[...])
-
-    def attend(j):
-        scores = nt_dot(qp[j], kn[...])
-        before = top[j][:, :1]
-        peak = jnp.maximum(before, jnp.max(scores, axis=1, keepdims=True))
+        qp[pair, :, at * n : (at + 1) * n] = (nt_dot(wp[1], query) * scale).astype(jnp.bfloat16)
+
+    def clear(pair):
+        top[pair] = jnp.full((1, 2 * n), -jnp.inf, jnp.float32)
+        low[pair] = jnp.zeros((1, 2 * n), jnp.float32)
+        acc[pair] = jnp.zeros((C, 2 * n), jnp.float32)
+
+    def prepare(core, source, values):
+        keys = normed(values)
+        kn[core, source] = keys
+        kt[core, source] = jnp.transpose(keys)
+
+    def attend(pair, core, source):
+        scores = nn_dot(kn[core, source], qp[pair])
+        before = top[pair]
+        peak = jnp.maximum(before, jnp.max(scores, axis=0, keepdims=True))
         expo = jnp.exp2(scores - peak).astype(jnp.bfloat16)
         fade = jnp.exp2(before - peak)
-        sums = low[j][:, :1] * fade + jnp.sum(expo.astype(jnp.float32), axis=1, keepdims=True)
-        top[j] = jnp.broadcast_to(peak, (n, LANES))
-        low[j] = jnp.broadcast_to(sums, (n, LANES))
-        acc[j] = acc[j] * fade + nn_dot(expo, kn[...])
-
-    c_copy(0, res).wait()
-    kn[0:n] = normed(res[...])
-    kn[n : 2 * n] = normed(kv[1, 0])
-    attend(0)
-
-    def q_finish(j, carry):
-        q_copy(j).wait()
-        make_query(j, qn[j])
-        attend(j)
+        top[pair] = peak
+        low[pair] = low[pair] * fade + jnp.sum(
+            expo.astype(jnp.float32), axis=0, keepdims=True
+        )
+        acc[pair] = acc[pair] * fade + nn_dot(kt[core, source], expo)
+
+    def columns(fn, distances, inner):
+        for distance in distances:
+            for way in (0, 1):
+                source = head + (distance if way else -distance)
+                chosen = reachable(way, distance)
+                if inner is not None:
+                    within = jnp.logical_and(source > 0, source < heads - 1)
+                    chosen = jnp.logical_and(chosen, within if inner else ~within)
+
+                @pl.when(chosen)
+                def _(distance=distance, way=way, source=source):
+                    fn(source, distance, way)
+
+    far = tuple(range(2, heads))
+
+    def pass_on(ch):
+        def go(copy):
+            copy.wait_recv()
+            copy.start()
+
+        with jax.named_scope("relay"):
+            for distance in range(DIRECT, heads - 1):
+                onward(distance, go, (ch,))
+
+    with jax.named_scope("query0"):
+        clear(0)
+        make_query(0, 0, res[...])
+        prepare(0, head, res[...])
+    with jax.named_scope("q_wait0"):
+        q_copy(1).wait()
+    for ch in range(CHUNKS - 1):
+        pass_on(ch)
+    with jax.named_scope("query1"):
+        make_query(0, 1, qn[1])
+    with jax.named_scope("attend_own"):
+        attend(0, 0, head)
+    with jax.named_scope("c_own"):
+        c_copy(head, res).wait()
+        prepare(1, head, kv[1, head])
+    with jax.named_scope("attend_partner"):
+        attend(0, 1, head)
+
+    def fetch(source, distance, way, work):
+        with jax.named_scope("z_wait"):
+            z_arrived(source, distance, way)
+            c_copy(source, kv.at[0, source]).start()
+        with jax.named_scope("z_attend0"):
+            prepare(0, source, kv[0, source])
+            work(0, source)
+        with jax.named_scope("c_wait"):
+            c_copy(source, kv.at[0, source]).wait()
+        with jax.named_scope("z_attend1"):
+            prepare(1, source, kv[1, source])
+            work(1, source)
+
+    def near(source, distance, way):
+        fetch(source, distance, way, lambda core, place: attend(0, core, place))
+
+    def far_pairs(core, source):
+        def one(pair, carry):
+            attend(pair, core, source)
+            return carry
+
+        if pairs == 2:
+            attend(1, core, source)
+        else:
+            lax.fori_loop(1, pairs, one, 0)
+
+    pass_on(CHUNKS - 1)
+    columns(near, (1,), True)
+
+    def rest(pair, carry):
+        with jax.named_scope("q_wait1"):
+            for at in range(2):
+                q_copy(2 * pair + at).wait()
+        with jax.named_scope("query2"):
+            clear(pair)
+            for at in range(2):
+                make_query(pair, at, qn[2 * pair + at])
+        with jax.named_scope("attend_rest"):
+            attend(pair, 0, head)
+            attend(pair, 1, head)
         return carry
 
-    lax.fori_loop(1, half, q_finish, 0)
-
-    def column(k, carry):
-        z_copy(k).wait()
-        c_copy(k, kv.at[0, k]).start()
-        kn[0:n] = normed(kv[0, k])
-        c_copy(k, kv.at[0, k]).wait()
-        kn[n : 2 * n] = normed(kv[1, k])
-
-        def one(j, inner):
-            attend(j)
-            return inner
-
-        lax.fori_loop(0, half, one, 0)
-        return carry
-
-    lax.fori_loop(1, heads, column, 0)
+    lax.fori_loop(1, pairs, rest, 0)
+
+    def again(source, distance, way):
+        with jax.named_scope("again"):
+            far_pairs(0, source)
+            far_pairs(1, source)
+
+    def late(*place):
+        fetch(*place, far_pairs)
+
+    columns(again, (1,), True)
+    columns(late, far, None)
+    columns(late, (1,), False)
 
     def give_copies(j):
         owner = (lax.rem(tile + tiles - 2 * j, tiles), head)
@@ -440,40 +564,64 @@
             remote(l_out.at[j], l_in.at[j], l_send.at[j], l_recv.at[j], owner),
         ]
 
-    def finish(j, o_to, l_to):
-        level = top[j] + jnp.log2(low[j])
-        l_to[j] = jnp.transpose(level)[:8]
-        o_to[j] = (acc[j] / low[j][:, :1]).astype(jnp.bfloat16)
-
-    def give(j, carry):
-        finish(j, o_out, l_out)
+    def finish(pair, at, o_to, l_to):
+        lanes = slice(at * n, (at + 1) * n)
+        sums = low[pair, :, lanes]
+        l_to[2 * pair + at] = top[pair, :, lanes] + jnp.log2(sums)
+        o_to[2 * pair + at] = (acc[pair, :, lanes] * (1.0 / sums)).astype(jnp.bfloat16)
+
+    def send(j):
         for copy in give_copies(j):
             copy.start()
+
+    def give(i, carry):
+        pair = pairs - 1 - i
+        for at in range(2):
+            finish(pair, at, o_out, l_out)
+            send(2 * pair + at)
         return carry
 
-    lax.fori_loop(1, half, give, 0)
-    finish(0, o_in, l_in)
+    with jax.named_scope("give"):
+        lax.fori_loop(0, pairs - 1, give, 0)
+
+    def own(source, distance, way):
+        with jax.named_scope("own_far"):
+            attend(0, 0, source)
+            attend(0, 1, source)
+
+    columns(own, far, None)
+    columns(own, (1,), False)
+    with jax.named_scope("give1"):
+        finish(0, 1, o_out, l_out)
+        send(1)
+    with jax.named_scope("finish0"):
+        finish(0, 0, o_in, l_in)
+        straight(lambda copy: copy.wait_send())
+        for distance in range(DIRECT, heads - 1):
+            onward(distance, lambda copy: copy.wait_send())
 
     def take(j, carry):
         for copy in give_copies(j):
             copy.wait()
         return carry
 
-    lax.fori_loop(1, half, take, 0)
-    peak = l_in[0]
-    for j in range(1, half):
-        peak = jnp.maximum(peak, l_in[j])
-    shares = [jnp.exp2(l_in[j] - peak) for j in range(half)]
-    whole = shares[0]
-    for j in range(1, half):
-        whole = whole + shares[j]
-    mixed = jnp.zeros((n, C), jnp.float32)
-    for j in range(half):
-        share = jnp.transpose(jnp.broadcast_to((shares[j] / whole)[:1], (LANES, n)))[:, :1]
-        mixed = mixed + share * o_in[j].astype(jnp.float32)
-    attended = (nn_dot(mixed.astype(jnp.bfloat16), wp[2]) + vb[...]).astype(jnp.bfloat16)
-    out = nn_dot(attended, wp[3]) + ob[...]
-    out_ref[...] = (res[...].astype(jnp.float32) + out).astype(jnp.bfloat16)
+    with jax.named_scope("take"):
+        lax.fori_loop(1, half, take, 0)
+    with jax.named_scope("last"):
+        peak = l_in[0]
+        for j in range(1, half):
+            peak = jnp.maximum(peak, l_in[j])
+        shares = [jnp.exp2(l_in[j] - peak) for j in range(half)]
+        whole = shares[0]
+        for j in range(1, half):
+            whole = whole + shares[j]
+        mixed = jnp.zeros((C, n), jnp.float32)
+        for j in range(half):
+            mixed = mixed + (shares[j] / whole) * o_in[j].astype(jnp.float32)
+        mixed = jnp.transpose(mixed.astype(jnp.bfloat16))
+        attended = (nn_dot(mixed, wp[2]) + vb[...]).astype(jnp.bfloat16)
+        out = nn_dot(attended, wp[3]) + ob[...]
+        out_ref[...] = (res[...].astype(jnp.float32) + out).astype(jnp.bfloat16)
 
 
 def per_device(
@@ -529,10 +677,12 @@
     dma = pltpu.SemaphoreType.DMA
     out = pl.pallas_call(
         functools.partial(block_kernel, tiles, heads),
-        out_shape=jax.ShapeDtypeStruct((n, C), bf16),
-        in_specs=[VMEM] * (1 + len(vectors)) + [ANY] * len(matrices),
+        out_shape=pltpu.VMEM((n, C), bf16),
+        in_specs=[HBM] * (1 + len(vectors) + len(matrices)),
         out_specs=VMEM,
         scratch_shapes=[
+            pltpu.VMEM((rows, cols, C), bf16),
+            pltpu.VMEM((len(vectors), 1, C), f32),
             pltpu.VMEM((9 * C, C), bf16),
             pltpu.VMEM((9 * C, C), bf16),
             pltpu.VMEM((4, C, C), bf16),
@@ -549,23 +699,26 @@
             pltpu.VMEM((8, C), f32),
             pltpu.VMEM((n, C), bf16),
             pltpu.VMEM((2, heads, n, C), bf16),
-            pltpu.VMEM((2 * n, C), bf16),
+            pltpu.VMEM((2, heads, n, C), bf16),
+            pltpu.VMEM((2, heads, C, n), bf16),
             pltpu.VMEM((half, n, C), bf16),
-            pltpu.VMEM((half, n, C), bf16),
-            pltpu.VMEM((half, n, C), f32),
-            pltpu.VMEM((half, n, LANES), f32),
-            pltpu.VMEM((half, n, LANES), f32),
-            pltpu.VMEM((half, n, C), bf16),
-            pltpu.VMEM((half, n, C), bf16),
-            pltpu.VMEM((half, 8, n), f32),
-            pltpu.VMEM((half, 8, n), f32),
-            dma((6,)),
-            dma((3, total)),
-            dma((3, total)),
+            pltpu.VMEM((half // 2, C, 2 * n), bf16),
+            pltpu.VMEM((half // 2, C, 2 * n), f32),
+            pltpu.VMEM((half // 2, 1, 2 * n), f32),
+            pltpu.VMEM((half // 2, 1, 2 * n), f32),
+            pltpu.VMEM((half, C, n), bf16),
+            pltpu.VMEM((half, C, n), bf16),
+            pltpu.VMEM((half, 1, n), f32),
+            pltpu.VMEM((half, 1, n), f32),
+            dma,
+            dma((len(vectors),)),
+            dma((len(matrices),)),
+            dma((3,)),
+            dma((3,)),
             dma((2, 8)),
             dma((2, 8)),
-            dma((heads,)),
-            dma((heads,)),
+            dma((2, heads, CHUNKS)),
+            dma((heads, CHUNKS)),
             dma((heads,)),
             dma((heads,)),
             dma((half,)),
@@ -575,7 +728,9 @@
             dma((half,)),
             dma((half,)),
         ],
-        compiler_params=pltpu.CompilerParams(collective_id=1, has_side_effects=True),
+        compiler_params=pltpu.CompilerParams(
+            collective_id=1, has_side_effects=True, vmem_limit_bytes=VMEM_LIMIT
+        ),
         name="middle_block",
     )(latent, *vectors, *matrices)
     return out.reshape(rows, cols, C)

time: 76.3 us -> 63.3 us (0.83)
  Pallas kernels: 74.4 us -> 62.5 us
  local copies, waits for them, and re-layouts: 1.67 us -> 0.71 us
    pallas_call x1, Pallas kernels: 74.4 us -> 62.5 us  [per_device(): pl.pallas_call(functools.partial(block_kernel, tiles, heads), out_shape=p...]
    unnamed x1, local copies, waits for them, and re-layouts: 1.67 us -> 0.71 us
where the time goes in v2:
time: 63.3 us; the launch traced here: 63.2 us
  Pallas kernels  62.5 us (99%)
  local copies, waits for them, and re-layouts  0.71 us (1%)
    pallas_call x1, Pallas kernels, per_device(): pl.pallas_call(functools.partial(block_kernel, tiles, heads), out_shape=p...  62.5 us

profile of v2, /device:TPU:0, one launch (start us, length us, event | category | flops | bytes accessed | tf_op | source)
XLA Modules:
  0.0 63.2 jit_solution(9342164192592614646)
XLA Ops:
  0.0 62.5 %middle_block.1 = bf16[256,512]{1,0:T(8,128)(2,1)S(1)} custom-call(bf16[2,128,512]{2,1,0:T(8,128)(2,1)} %lat_hbm.1, f32[1,512]{1,0:T(1,128)} %bitcast.17, f32[1,512]{1,0:T(1,128)} %bitcast.18, f32[1,512]{1,0:T(1,128)} %bitcast.19, f32[1,512]{1,0:T(1,128)} %bitcast.20, f32[1,512]{1,0:T(1,128)} %bitcast.21, f32[1,512]{1,0:T(1,128)} %bitcast.22, ...), custom_call_target="tpu_custom_call" | custom-call | tf_op jit(solution)/shard_map/middle_block/pallas_call | solution.py:678
  62.5 0.7 %copy.20 = bf16[2,128,512]{2,1,0:T(8,128)(2,1)} copy(bf16[2,128,512]{2,1,0:T(8,128)(2,1)S(1)} %bitcast.14) | data formatting | bytes 524288

commit v3 on v2

--- a/solution.py
+++ b/solution.py
@@ -21,7 +21,8 @@
 VMEM = pl.BlockSpec(memory_space=pltpu.VMEM)
 HBM = pl.BlockSpec(memory_space=pltpu.HBM)
 VECTORS = 11
-CHUNKS = 2
+CHUNKS = 4
+SPLIT = 1
 DIRECT = 2
 VMEM_LIMIT = 56 * 1024 * 1024
 
@@ -38,13 +39,16 @@
     return lax.broadcasted_iota(jnp.int32, (rows, LANES), 1)
 
 
+def lane_partner(values, step):
+    below = pltpu.roll(values, step, 1)
+    above = pltpu.roll(values, LANES - step, 1)
+    return jnp.where(lane_index(values.shape[0]) % (2 * step) >= step, below, above)
+
+
 def group_sum(values):
-    lane = lane_index(values.shape[0])
     step = 1
     while step < WIDTH:
-        below = pltpu.roll(values, step, 1)
-        above = pltpu.roll(values, LANES - step, 1)
-        values = values + jnp.where(lane % (2 * step) >= step, below, above)
+        values = values + lane_partner(values, step)
         step *= 2
     return values
 
@@ -62,10 +66,14 @@
     mean = jnp.sum(values, axis=0, keepdims=True) / count
     deviation = values - mean
     square = jnp.sum(deviation * deviation, axis=0, keepdims=True)
-    mean, square = fold(mean), fold(square)
-    group_mean = group_sum(mean) / WIDTH
-    gap = mean - group_mean
-    square = group_sum(square + count * gap * gap)
+    group_mean, square = fold(mean), fold(square)
+    step = 1
+    while step < WIDTH:
+        other = lane_partner(group_mean, step)
+        gap = group_mean - other
+        square = square + lane_partner(square, step) + (0.5 * count * step) * (gap * gap)
+        group_mean = 0.5 * (group_mean + other)
+        step *= 2
     lane = lane_index(1)
     packed = jnp.zeros((1, LANES), jnp.float32)
     for i in range(PARTS):
@@ -91,7 +99,8 @@
 
 
 def silu(values):
-    return values / (1.0 + jnp.exp(-values))
+    half = 0.5 * values
+    return half + half * jnp.tanh(half)
 
 
 def block_kernel(
@@ -132,6 +141,10 @@
         o_in,
         l_out,
         l_in,
+        u_in,
+        ul_in,
+        m_out,
+        ml_out,
         lat_sem,
         v_sem,
         w_sem,
@@ -159,12 +172,25 @@
     me = tile * heads + head
     partner = (tile + 1 - 2 * lax.rem(tile, 2), head)
 
+    def fellow(j):
+        chip, bit, other = lax.div(tile, 2), 1, 0
+        if half & (half - 1):
+            return lax.rem(tile + 2 * j, tiles)
+        while bit < half:
+            mine, flip = lax.rem(lax.div(chip, bit), 2), (j // bit) % 2
+            other = other + bit * (mine + flip - 2 * mine * flip)
+            bit *= 2
+        return 2 * other + lax.rem(tile, 2)
+
+    def lender(j):
+        return fellow(j) if half & (half - 1) == 0 else lax.rem(tile + tiles - 2 * j, tiles)
+
     barrier = pltpu.get_barrier_semaphore()
 
     def greet(k, carry):
         peer = lax.rem(me + k, total)
         pl.semaphore_signal(
-            barrier, inc=1, device_id=(peer // heads, lax.rem(peer, heads)), device_id_type=MESH
+            barrier, inc=1, device_id=(lax.div(peer, heads), lax.rem(peer, heads)), device_id_type=MESH
         )
         return carry
 
@@ -200,7 +226,7 @@
             stat_in.at[phase, k],
             s_send.at[phase],
             s_recv.at[phase],
-            (peer // heads, lax.rem(peer, heads)),
+            (lax.div(peer, heads), lax.rem(peer, heads)),
         )
 
     def stats_start(phase):
@@ -376,15 +402,15 @@
 
     def straight(fn):
         at_end = jnp.logical_or(head == 0, head == heads - 1)
-        farther = tuple(range(2, min(DIRECT, heads - 1) + 1))
-        for distances, chosen in ((farther, at_end), ((1,), True), (farther, ~at_end)):
-            for distance in distances:
-                for ch in range(CHUNKS):
-                    for way in (0, 1):
-
-                        @pl.when(jnp.logical_and(reachable(way, distance), chosen))
-                        def _(way=way, distance=distance, ch=ch):
-                            fn(z_copy(head, res, way, distance, ch))
+        farther = [(d, c) for d in range(2, min(DIRECT, heads - 1) + 1) for c in range(CHUNKS)]
+        nearer = [(1, c) for c in range(CHUNKS)]
+        for chosen, order in ((at_end, farther + nearer), (~at_end, nearer + farther)):
+            for distance, ch in order:
+                for way in (0, 1):
+
+                    @pl.when(jnp.logical_and(reachable(way, distance), chosen))
+                    def _(way=way, distance=distance, ch=ch):
+                        fn(z_copy(head, res, way, distance, ch))
 
     def onward(distance, fn, chunks=tuple(range(CHUNKS))):
         for ch in chunks:
@@ -395,10 +421,9 @@
                     source = head + (-distance if way else distance)
                     fn(z_copy(source, kv.at[0, source], way, distance + 1, ch))
 
-    def z_arrived(source, distance, way):
+    def z_arrived(source, distance, way, ch):
         def wait():
-            for ch in range(CHUNKS):
-                z_copy(source, res, way, 1, ch).wait_recv()
+            z_copy(source, res, way, 1, ch).wait_recv()
 
         if heads - 1 > DIRECT:
             passed = jnp.logical_and(distance >= DIRECT, reachable(1 - way, 1))
@@ -406,24 +431,39 @@
         else:
             wait()
 
-    def c_copy(source, src):
+    def c_copy(source, src, ch):
         return remote(
-            src, kv.at[1, source], c_send.at[source], c_recv.at[source], partner
+            piece(src, ch),
+            piece(kv.at[1, source], ch),
+            c_send.at[source, ch],
+            c_recv.at[source, ch],
+            partner,
         )
 
     def q_copy(j):
         return remote(
-            res, qn.at[j], q_send.at[j], q_recv.at[j], (lax.rem(tile + 2 * j, tiles), head)
+            res, qn.at[j], q_send.at[j], q_recv.at[j], (fellow(j), head)
         )
 
     def q_begin(j, carry):
         q_copy(j).start()
         return carry
 
-    c_copy(head, res).start()
+    for ch in range(CHUNKS):
+        c_copy(head, res, ch).start()
+    def pass_on(ch):
+        def go(copy):
+            copy.wait_recv()
+            copy.start()
+
+        with jax.named_scope("relay"):
+            for distance in range(DIRECT, heads - 1):
+                onward(distance, go, (ch,))
+
+    straight(lambda copy: copy.start())
+    lax.fori_loop(1, half, q_begin, 0)
+    pass_on(0)
     with jax.named_scope("norm2"):
-        straight(lambda copy: copy.start())
-        lax.fori_loop(1, half, q_begin, 0)
         stats_finish(2, n3g, n3s)
         for copy in weights[2:]:
             copy.wait()
@@ -444,22 +484,39 @@
 
     def prepare(core, source, values):
         keys = normed(values)
-        kn[core, source] = keys
-        kt[core, source] = jnp.transpose(keys)
-
-    def attend(pair, core, source):
-        scores = nn_dot(kn[core, source], qp[pair])
-        before = top[pair]
-        peak = jnp.maximum(before, jnp.max(scores, axis=0, keepdims=True))
-        expo = jnp.exp2(scores - peak).astype(jnp.bfloat16)
+        kn[source, core] = keys
+        kt[source, :, core * n : (core + 1) * n] = jnp.transpose(keys)
+
+    def one_core(core, source):
+        return kn.at[source, core], kt.at[source, :, pl.ds(core * n, n)]
+
+    def both_cores(source):
+        return kn.at[source], kt.at[source]
+
+    def attend(pair, *blocks):
+        for at in range(SPLIT):
+            width = 2 * n // SPLIT
+            attend_lanes(pair, slice(at * width, (at + 1) * width), blocks)
+
+    def attend_lanes(pair, lanes, blocks):
+        query = qp[pair, :, lanes]
+        scores = [nn_dot(keys[...].reshape(-1, C), query) for keys, _ in blocks]
+        before = top[pair, :, lanes]
+        peak = before
+        for one in scores:
+            peak = jnp.maximum(peak, jnp.max(one, axis=0, keepdims=True))
         fade = jnp.exp2(before - peak)
-        top[pair] = peak
-        low[pair] = low[pair] * fade + jnp.sum(
-            expo.astype(jnp.float32), axis=0, keepdims=True
-        )
-        acc[pair] = acc[pair] * fade + nn_dot(kt[core, source], expo)
-
-    def columns(fn, distances, inner):
+        sums, values = low[pair, :, lanes] * fade, None
+        for one, (_, turned) in zip(scores, blocks):
+            expo = jnp.exp2(one - peak).astype(jnp.bfloat16)
+            sums = sums + jnp.sum(expo.astype(jnp.float32), axis=0, keepdims=True)
+            part = nn_dot(turned[...], expo)
+            values = part if values is None else values + part
+        top[pair, :, lanes] = peak
+        low[pair, :, lanes] = sums
+        acc[pair, :, lanes] = acc[pair, :, lanes] * fade + values
+
+    def columns(fn, distances, inner=None, extra=None):
         for distance in distances:
             for way in (0, 1):
                 source = head + (distance if way else -distance)
@@ -467,68 +524,64 @@
                 if inner is not None:
                     within = jnp.logical_and(source > 0, source < heads - 1)
                     chosen = jnp.logical_and(chosen, within if inner else ~within)
+                if extra is not None:
+                    chosen = jnp.logical_and(chosen, extra)
 
                 @pl.when(chosen)
                 def _(distance=distance, way=way, source=source):
                     fn(source, distance, way)
 
     far = tuple(range(2, heads))
-
-    def pass_on(ch):
-        def go(copy):
-            copy.wait_recv()
-            copy.start()
-
-        with jax.named_scope("relay"):
-            for distance in range(DIRECT, heads - 1):
-                onward(distance, go, (ch,))
+    at_end = jnp.logical_or(head == 0, head == heads - 1)
 
     with jax.named_scope("query0"):
         clear(0)
         make_query(0, 0, res[...])
         prepare(0, head, res[...])
+    pass_on(1)
     with jax.named_scope("q_wait0"):
         q_copy(1).wait()
-    for ch in range(CHUNKS - 1):
-        pass_on(ch)
     with jax.named_scope("query1"):
         make_query(0, 1, qn[1])
+        for ch in range(CHUNKS):
+            c_copy(head, res, ch).wait()
+        prepare(1, head, kv[1, head])
+    pass_on(2)
     with jax.named_scope("attend_own"):
-        attend(0, 0, head)
-    with jax.named_scope("c_own"):
-        c_copy(head, res).wait()
-        prepare(1, head, kv[1, head])
-    with jax.named_scope("attend_partner"):
-        attend(0, 1, head)
-
-    def fetch(source, distance, way, work):
+        attend(0, both_cores(head))
+    pass_on(3)
+
+    def begin(source, distance, way):
         with jax.named_scope("z_wait"):
-            z_arrived(source, distance, way)
-            c_copy(source, kv.at[0, source]).start()
-        with jax.named_scope("z_attend0"):
+            for ch in range(CHUNKS):
+                z_arrived(source, distance, way, ch)
+                c_copy(source, kv.at[0, source], ch).start()
+        with jax.named_scope("prepare0"):
             prepare(0, source, kv[0, source])
-            work(0, source)
+
+    def second(source):
         with jax.named_scope("c_wait"):
-            c_copy(source, kv.at[0, source]).wait()
-        with jax.named_scope("z_attend1"):
+            for ch in range(CHUNKS):
+                c_copy(source, kv.at[0, source], ch).wait()
+        with jax.named_scope("prepare1"):
             prepare(1, source, kv[1, source])
-            work(1, source)
-
-    def near(source, distance, way):
-        fetch(source, distance, way, lambda core, place: attend(0, core, place))
-
-    def far_pairs(core, source):
+
+    def other_pairs(*blocks):
         def one(pair, carry):
-            attend(pair, core, source)
+            attend(pair, *blocks)
             return carry
 
         if pairs == 2:
-            attend(1, core, source)
+            attend(1, *blocks)
         else:
             lax.fori_loop(1, pairs, one, 0)
 
-    pass_on(CHUNKS - 1)
-    columns(near, (1,), True)
+    def together(source, distance, way):
+        second(source)
+        with jax.named_scope("together"):
+            other_pairs(both_cores(source))
+
+    columns(begin, (1,), True)
 
     def rest(pair, carry):
         with jax.named_scope("q_wait1"):
@@ -539,85 +592,163 @@
             for at in range(2):
                 make_query(pair, at, qn[2 * pair + at])
         with jax.named_scope("attend_rest"):
-            attend(pair, 0, head)
-            attend(pair, 1, head)
+            attend(pair, both_cores(head))
         return carry
 
     lax.fori_loop(1, pairs, rest, 0)
-
-    def again(source, distance, way):
-        with jax.named_scope("again"):
-            far_pairs(0, source)
-            far_pairs(1, source)
-
-    def late(*place):
-        fetch(*place, far_pairs)
-
-    columns(again, (1,), True)
-    columns(late, far, None)
-    columns(late, (1,), False)
+    columns(begin, (2,), extra=~at_end)
+    columns(together, (1,), True)
+    columns(begin, (1,), False)
+    columns(together, (2,), extra=~at_end)
+    columns(together, (1,), False)
+    def first_half(source, distance, way):
+        begin(source, distance, way)
+        with jax.named_scope("late0"):
+            other_pairs(one_core(0, source))
+        second(source)
+
+    def second_half(source, distance, way):
+        with jax.named_scope("late1"):
+            other_pairs(one_core(1, source))
+
+    columns(first_half, (2,), extra=at_end)
+    columns(begin, far[1:])
+    columns(second_half, (2,), extra=at_end)
+    columns(together, far[1:])
+
+    def both(src, dst, src_level, dst_level, sem, device):
+        return [
+            remote(src, dst, o_send.at[sem], o_recv.at[sem], device),
+            remote(src_level, dst_level, l_send.at[sem], l_recv.at[sem], device),
+        ]
 
     def give_copies(j):
-        owner = (lax.rem(tile + tiles - 2 * j, tiles), head)
-        return [
-            remote(o_out.at[j], o_in.at[j], o_send.at[j], o_recv.at[j], owner),
-            remote(l_out.at[j], l_in.at[j], l_send.at[j], l_recv.at[j], owner),
-        ]
+        return both(o_out.at[j], o_in.at[j], l_out.at[j], l_in.at[j], j, (lender(j), head))
 
     def finish(pair, at, o_to, l_to):
-        lanes = slice(at * n, (at + 1) * n)
-        sums = low[pair, :, lanes]
-        l_to[2 * pair + at] = top[pair, :, lanes] + jnp.log2(sums)
-        o_to[2 * pair + at] = (acc[pair, :, lanes] * (1.0 / sums)).astype(jnp.bfloat16)
-
-    def send(j):
-        for copy in give_copies(j):
-            copy.start()
-
-    def give(i, carry):
-        pair = pairs - 1 - i
-        for at in range(2):
-            finish(pair, at, o_out, l_out)
-            send(2 * pair + at)
-        return carry
-
-    with jax.named_scope("give"):
-        lax.fori_loop(0, pairs - 1, give, 0)
+        for part in range(2):
+            lanes = slice((2 * at + part) * (n // 2), (2 * at + part + 1) * (n // 2))
+            sums = low[pair, :, lanes]
+            l_to[2 * pair + at, part] = top[pair, :, lanes] + jnp.log2(sums)
+            o_to[2 * pair + at, part] = (acc[pair, :, lanes] * (1.0 / sums)).astype(jnp.bfloat16)
 
     def own(source, distance, way):
         with jax.named_scope("own_far"):
-            attend(0, 0, source)
-            attend(0, 1, source)
-
-    columns(own, far, None)
-    columns(own, (1,), False)
-    with jax.named_scope("give1"):
-        finish(0, 1, o_out, l_out)
-        send(1)
-    with jax.named_scope("finish0"):
-        finish(0, 0, o_in, l_in)
+            attend(0, both_cores(source))
+
+    def column_sent():
         straight(lambda copy: copy.wait_send())
         for distance in range(DIRECT, heads - 1):
             onward(distance, lambda copy: copy.wait_send())
 
-    def take(j, carry):
-        for copy in give_copies(j):
+    def begin_all(copies):
+        for copy in copies:
+            copy.start()
+
+    def end_all(copies):
+        for copy in copies:
             copy.wait()
-        return carry
-
-    with jax.named_scope("take"):
+
+    if half == 4:
+        def hop(part):
+            via = (fellow(2 - part), head)
+            return both(
+                o_out.at[3, part], u_in.at[part], l_out.at[3, part], ul_in.at[part], part, via
+            )
+
+        def direct(j):
+            part = 2 - j
+            return both(
+                o_out.at[j, part],
+                o_in.at[j, part],
+                l_out.at[j, part],
+                l_in.at[j, part],
+                1 + j,
+                (fellow(j), head),
+            )
+
+        def merged(j):
+            part = j - 1
+            return both(
+                m_out.at[part],
+                o_in.at[j, part],
+                ml_out.at[part],
+                l_in.at[j, part],
+                3 + j,
+                (fellow(j), head),
+            )
+
+        def merge(j):
+            part = j - 1
+            end_all(hop(part))
+            mine, theirs = l_out[j, part], ul_in[part]
+            level = jnp.maximum(mine, theirs)
+            keep, add = jnp.exp2(mine - level), jnp.exp2(theirs - level)
+            whole = keep + add
+            ml_out[part] = level + jnp.log2(whole)
+            values = o_out[j, part].astype(jnp.float32) * (keep / whole)
+            values = values + u_in[part].astype(jnp.float32) * (add / whole)
+            m_out[part] = values.astype(jnp.bfloat16)
+            begin_all(merged(j))
+
+        with jax.named_scope("give"):
+            finish(1, 1, o_out, l_out)
+            begin_all(hop(0))
+            begin_all(hop(1))
+            finish(1, 0, o_out, l_out)
+            begin_all(direct(2))
+        columns(own, tuple(range(1, heads)))
+        with jax.named_scope("give1"):
+            finish(0, 1, o_out, l_out)
+            begin_all(direct(1))
+        with jax.named_scope("finish0"):
+            finish(0, 0, o_in, l_in)
+            column_sent()
+        with jax.named_scope("merge2"):
+            merge(2)
+        with jax.named_scope("merge1"):
+            merge(1)
+        with jax.named_scope("take"):
+            for j in (1, 2):
+                end_all(direct(j))
+                end_all(merged(j))
+        parts = 3
+    else:
+
+        def give(i, carry):
+            pair = pairs - 1 - i
+            for at in range(2):
+                finish(pair, at, o_out, l_out)
+                begin_all(give_copies(2 * pair + at))
+            return carry
+
+        def take(j, carry):
+            end_all(give_copies(j))
+            return carry
+
+        lax.fori_loop(0, pairs - 1, give, 0)
+        columns(own, tuple(range(1, heads)))
+        finish(0, 1, o_out, l_out)
+        begin_all(give_copies(1))
+        finish(0, 0, o_in, l_in)
+        column_sent()
         lax.fori_loop(1, half, take, 0)
+        parts = half
     with jax.named_scope("last"):
-        peak = l_in[0]
-        for j in range(1, half):
-            peak = jnp.maximum(peak, l_in[j])
-        shares = [jnp.exp2(l_in[j] - peak) for j in range(half)]
-        whole = shares[0]
-        for j in range(1, half):
-            whole = whole + shares[j]
-        mixed = jnp.zeros((C, n), jnp.float32)
-        for j in range(half):
-            mixed = mixed + (shares[j] / whole) * o_in[j].astype(jnp.float32)
+        sides = []
+        for part in range(2):
+            peak = l_in[0, part]
+            for j in range(1, parts):
+                peak = jnp.maximum(peak, l_in[j, part])
+            shares = [jnp.exp2(l_in[j, part] - peak) for j in range(parts)]
+            whole = shares[0]
+            for j in range(1, parts):
+                whole = whole + shares[j]
+            side = jnp.zeros((C, n // 2), jnp.float32)
+            for j in range(parts):
+                side = side + (shares[j] / whole) * o_in[j, part].astype(jnp.float32)
+            sides.append(side)
+        mixed = jnp.concatenate(sides, axis=1)
         mixed = jnp.transpose(mixed.astype(jnp.bfloat16))
         attended = (nn_dot(mixed, wp[2]) + vb[...]).astype(jnp.bfloat16)
         out = nn_dot(attended, wp[3]) + ob[...]
@@ -699,17 +830,21 @@
             pltpu.VMEM((8, C), f32),
             pltpu.VMEM((n, C), bf16),
             pltpu.VMEM((2, heads, n, C), bf16),
-            pltpu.VMEM((2, heads, n, C), bf16),
-            pltpu.VMEM((2, heads, C, n), bf16),
+            pltpu.VMEM((heads, 2, n, C), bf16),
+            pltpu.VMEM((heads, C, 2 * n), bf16),
             pltpu.VMEM((half, n, C), bf16),
             pltpu.VMEM((half // 2, C, 2 * n), bf16),
             pltpu.VMEM((half // 2, C, 2 * n), f32),
             pltpu.VMEM((half // 2, 1, 2 * n), f32),
             pltpu.VMEM((half // 2, 1, 2 * n), f32),
-            pltpu.VMEM((half, C, n), bf16),
-            pltpu.VMEM((half, C, n), bf16),
-            pltpu.VMEM((half, 1, n), f32),
-            pltpu.VMEM((half, 1, n), f32),
+            pltpu.VMEM((half, 2, C, n // 2), bf16),
+            pltpu.VMEM((half, 2, C, n // 2), bf16),
+            pltpu.VMEM((half, 2, 1, n // 2), f32),
+            pltpu.VMEM((half, 2, 1, n // 2), f32),
+            pltpu.VMEM((2, C, n // 2), bf16),
+            pltpu.VMEM((2, 1, n // 2), f32),
+            pltpu.VMEM((2, C, n // 2), bf16),
+            pltpu.VMEM((2, 1, n // 2), f32),
             dma,
             dma((len(vectors),)),
             dma((len(matrices),)),
@@ -719,14 +854,14 @@
             dma((2, 8)),
             dma((2, heads, CHUNKS)),
             dma((heads, CHUNKS)),
-            dma((heads,)),
-            dma((heads,)),
+            dma((heads, CHUNKS)),
+            dma((heads, CHUNKS)),
             dma((half,)),
             dma((half,)),
-            dma((half,)),
-            dma((half,)),
-            dma((half,)),
-            dma((half,)),
+            dma((half + 2,)),
+            dma((half + 2,)),
+            dma((half + 2,)),
+            dma((half + 2,)),
         ],
         compiler_params=pltpu.CompilerParams(
             collective_id=1, has_side_effects=True, vmem_limit_bytes=VMEM_LIMIT

time: 63.3 us -> 59.7 us (0.943)
  Pallas kernels: 62.5 us -> 58.9 us
    pallas_call x1, Pallas kernels: 62.5 us -> 58.9 us  [per_device(): pl.pallas_call(functools.partial(block_kernel, tiles, heads), out_shape=p...]
where the time goes in v3:
time: 59.7 us; the launch traced here: 59.6 us
  Pallas kernels  58.9 us (99%)
  local copies, waits for them, and re-layouts  0.71 us (1%)
    pallas_call x1, Pallas kernels, per_device(): pl.pallas_call(functools.partial(block_kernel, tiles, heads), out_shape=p...  58.9 us

profile of v3, /device:TPU:0, one launch (start us, length us, event | category | flops | bytes accessed | tf_op | source)
XLA Modules:
  0.0 59.6 jit_solution(8332581808650671434)
XLA Ops:
  0.0 58.9 %middle_block.1 = bf16[256,512]{1,0:T(8,128)(2,1)S(1)} custom-call(bf16[2,128,512]{2,1,0:T(8,128)(2,1)} %lat_hbm.1, f32[1,512]{1,0:T(1,128)} %bitcast.17, f32[1,512]{1,0:T(1,128)} %bitcast.18, f32[1,512]{1,0:T(1,128)} %bitcast.19, f32[1,512]{1,0:T(1,128)} %bitcast.20, f32[1,512]{1,0:T(1,128)} %bitcast.21, f32[1,512]{1,0:T(1,128)} %bitcast.22, ...), custom_call_target="tpu_custom_call" | custom-call | tf_op jit(solution)/shard_map/middle_block/pallas_call | solution.py:809
  58.9 0.7 %copy.20 = bf16[2,128,512]{2,1,0:T(8,128)(2,1)} copy(bf16[2,128,512]{2,1,0:T(8,128)(2,1)S(1)} %bitcast.14) | data formatting | bytes 524288

commit v4 on v3

--- a/solution.py
+++ b/solution.py
@@ -22,9 +22,16 @@
 HBM = pl.BlockSpec(memory_space=pltpu.HBM)
 VECTORS = 11
 CHUNKS = 4
-SPLIT = 1
 DIRECT = 2
 VMEM_LIMIT = 56 * 1024 * 1024
+
+
+def interleaved(far, near):
+    order, rest, near = far[: len(far) // 2], far[len(far) // 2 :], list(near)
+    for place in rest:
+        order += near[:1] + [place]
+        near = near[1:]
+    return order + near
 
 
 def nt_dot(a, b):
@@ -339,13 +346,13 @@
 
     with jax.named_scope("stats0"):
         latent_copy.wait()
-        put_columns(0, lat_ref[...].astype(jnp.float32))
         put_stats(0, lat_ref[...].astype(jnp.float32).reshape(n, C))
     with jax.named_scope("barrier"):
         pl.semaphore_wait(barrier, total - 1)
     with jax.named_scope("send0"):
         plan = halo_plan(0, lat_ref.at[0], lat_ref.at[rows - 1])
         stats_start(0)
+        put_columns(0, lat_ref[...].astype(jnp.float32))
         halo_start(0, plan)
     with jax.named_scope("halo0"):
         halo_finish(0, plan)
@@ -362,12 +369,12 @@
 
     with jax.named_scope("stats1"):
         put_stats(1, hid[...].reshape(n, C))
-        put_columns(1, hid[...])
-        row_out[0] = hid[0].astype(jnp.bfloat16)
-        row_out[1] = hid[rows - 1].astype(jnp.bfloat16)
     with jax.named_scope("send1"):
         plan = halo_plan(1, row_out.at[0], row_out.at[1])
         stats_start(1)
+        row_out[0] = hid[0].astype(jnp.bfloat16)
+        row_out[1] = hid[rows - 1].astype(jnp.bfloat16)
+        put_columns(1, hid[...])
         halo_start(1, plan)
     with jax.named_scope("halo1"):
         halo_finish(1, plan)
@@ -400,11 +407,12 @@
     def reachable(way, distance):
         return head + distance < heads if way else head - distance >= 0
 
+    at_end = jnp.logical_or(head == 0, head == heads - 1)
+
     def straight(fn):
-        at_end = jnp.logical_or(head == 0, head == heads - 1)
-        farther = [(d, c) for d in range(2, min(DIRECT, heads - 1) + 1) for c in range(CHUNKS)]
-        nearer = [(1, c) for c in range(CHUNKS)]
-        for chosen, order in ((at_end, farther + nearer), (~at_end, nearer + farther)):
+        nearer = [(1, ch) for ch in range(CHUNKS)]
+        farther = [(d, ch) for d in range(2, min(DIRECT, heads - 1) + 1) for ch in range(CHUNKS)]
+        for chosen, order in ((at_end, interleaved(farther, nearer)), (~at_end, farther + nearer)):
             for distance, ch in order:
                 for way in (0, 1):
 
@@ -451,6 +459,7 @@
 
     for ch in range(CHUNKS):
         c_copy(head, res, ch).start()
+
     def pass_on(ch):
         def go(copy):
             copy.wait_recv()
@@ -463,6 +472,7 @@
     straight(lambda copy: copy.start())
     lax.fori_loop(1, half, q_begin, 0)
     pass_on(0)
+    pass_on(1)
     with jax.named_scope("norm2"):
         stats_finish(2, n3g, n3s)
         for copy in weights[2:]:
@@ -494,62 +504,51 @@
         return kn.at[source], kt.at[source]
 
     def attend(pair, *blocks):
-        for at in range(SPLIT):
-            width = 2 * n // SPLIT
-            attend_lanes(pair, slice(at * width, (at + 1) * width), blocks)
-
-    def attend_lanes(pair, lanes, blocks):
-        query = qp[pair, :, lanes]
+        query = qp[pair]
         scores = [nn_dot(keys[...].reshape(-1, C), query) for keys, _ in blocks]
-        before = top[pair, :, lanes]
+        before = top[pair]
         peak = before
         for one in scores:
             peak = jnp.maximum(peak, jnp.max(one, axis=0, keepdims=True))
         fade = jnp.exp2(before - peak)
-        sums, values = low[pair, :, lanes] * fade, None
+        sums, values = low[pair] * fade, None
         for one, (_, turned) in zip(scores, blocks):
             expo = jnp.exp2(one - peak).astype(jnp.bfloat16)
             sums = sums + jnp.sum(expo.astype(jnp.float32), axis=0, keepdims=True)
             part = nn_dot(turned[...], expo)
             values = part if values is None else values + part
-        top[pair, :, lanes] = peak
-        low[pair, :, lanes] = sums
-        acc[pair, :, lanes] = acc[pair, :, lanes] * fade + values
-
-    def columns(fn, distances, inner=None, extra=None):
+        top[pair] = peak
+        low[pair] = sums
+        acc[pair] = acc[pair] * fade + values
+
+    def columns(fn, distances, chosen=None):
         for distance in distances:
             for way in (0, 1):
-                source = head + (distance if way else -distance)
-                chosen = reachable(way, distance)
-                if inner is not None:
-                    within = jnp.logical_and(source > 0, source < heads - 1)
-                    chosen = jnp.logical_and(chosen, within if inner else ~within)
-                if extra is not None:
-                    chosen = jnp.logical_and(chosen, extra)
-
-                @pl.when(chosen)
-                def _(distance=distance, way=way, source=source):
-                    fn(source, distance, way)
+                present = reachable(way, distance)
+                if chosen is not None:
+                    present = jnp.logical_and(present, chosen)
+
+                @pl.when(present)
+                def _(distance=distance, way=way):
+                    fn(head + (distance if way else -distance), distance, way)
 
     far = tuple(range(2, heads))
-    at_end = jnp.logical_or(head == 0, head == heads - 1)
 
     with jax.named_scope("query0"):
         clear(0)
         make_query(0, 0, res[...])
         prepare(0, head, res[...])
-    pass_on(1)
     with jax.named_scope("q_wait0"):
         q_copy(1).wait()
+    pass_on(2)
     with jax.named_scope("query1"):
         make_query(0, 1, qn[1])
         for ch in range(CHUNKS):
             c_copy(head, res, ch).wait()
         prepare(1, head, kv[1, head])
-    pass_on(2)
+    pass_on(3)
     with jax.named_scope("attend_own"):
         attend(0, both_cores(head))
-    pass_on(3)
 
     def begin(source, distance, way):
         with jax.named_scope("z_wait"):
@@ -581,7 +580,11 @@
         with jax.named_scope("together"):
             other_pairs(both_cores(source))
 
-    columns(begin, (1,), True)
+    def own(source, distance, way):
+        with jax.named_scope("own_far"):
+            attend(0, both_cores(source))
+
+    columns(begin, (1,), at_end)
 
     def rest(pair, carry):
         with jax.named_scope("q_wait1"):
@@ -591,30 +594,32 @@
             clear(pair)
             for at in range(2):
                 make_query(pair, at, qn[2 * pair + at])
-        with jax.named_scope("attend_rest"):
-            attend(pair, both_cores(head))
         return carry
 
     lax.fori_loop(1, pairs, rest, 0)
-    columns(begin, (2,), extra=~at_end)
-    columns(together, (1,), True)
-    columns(begin, (1,), False)
-    columns(together, (2,), extra=~at_end)
-    columns(together, (1,), False)
-    def first_half(source, distance, way):
-        begin(source, distance, way)
+    columns(begin, (2,), ~at_end)
+    with jax.named_scope("attend_rest"):
+        other_pairs(both_cores(head))
+    columns(begin, (2,), at_end)
+    columns(together, (1,), at_end)
+    columns(together, (2,))
+
+    def apart(*places):
+        sources = [source for source, _, _ in places]
+        for place in places:
+            begin(*place)
         with jax.named_scope("late0"):
-            other_pairs(one_core(0, source))
-        second(source)
-
-    def second_half(source, distance, way):
+            other_pairs(*[one_core(0, source) for source in sources])
+        for source in sources:
+            second(source)
         with jax.named_scope("late1"):
-            other_pairs(one_core(1, source))
-
-    columns(first_half, (2,), extra=at_end)
-    columns(begin, far[1:])
-    columns(second_half, (2,), extra=at_end)
-    columns(together, far[1:])
+            other_pairs(*[one_core(1, source) for source in sources])
+
+    @pl.when(~at_end)
+    def _():
+        apart((head - 1, 1, 0), (head + 1, 1, 1))
+
+    columns(lambda *place: apart(place), far[1:])
 
     def both(src, dst, src_level, dst_level, sem, device):
         return [
@@ -631,10 +636,6 @@
             sums = low[pair, :, lanes]
             l_to[2 * pair + at, part] = top[pair, :, lanes] + jnp.log2(sums)
             o_to[2 * pair + at, part] = (acc[pair, :, lanes] * (1.0 / sums)).astype(jnp.bfloat16)
-
-    def own(source, distance, way):
-        with jax.named_scope("own_far"):
-            attend(0, both_cores(source))
 
     def column_sent():
         straight(lambda copy: copy.wait_send())

time: 59.7 us -> 57.4 us (0.961)
  Pallas kernels: 58.9 us -> 56.6 us
    pallas_call x1, Pallas kernels: 58.9 us -> 56.6 us  [per_device(): pl.pallas_call(functools.partial(block_kernel, tiles, heads), out_shape=p...]
where the time goes in v4:
time: 57.4 us; the launch traced here: 57.3 us
  Pallas kernels  56.6 us (99%)
  local copies, waits for them, and re-layouts  0.71 us (1%)
    pallas_call x1, Pallas kernels, per_device(): pl.pallas_call(functools.partial(block_kernel, tiles, heads), out_shape=p...  56.6 us

profile of v4, /device:TPU:0, one launch (start us, length us, event | category | flops | bytes accessed | tf_op | source)
XLA Modules:
  0.0 57.3 jit_solution(10586518693899649220)
XLA Ops:
  0.0 56.6 %middle_block.1 = bf16[256,512]{1,0:T(8,128)(2,1)S(1)} custom-call(bf16[2,128,512]{2,1,0:T(8,128)(2,1)} %lat_hbm.1, f32[1,512]{1,0:T(1,128)} %bitcast.17, f32[1,512]{1,0:T(1,128)} %bitcast.18, f32[1,512]{1,0:T(1,128)} %bitcast.19, f32[1,512]{1,0:T(1,128)} %bitcast.20, f32[1,512]{1,0:T(1,128)} %bitcast.21, f32[1,512]{1,0:T(1,128)} %bitcast.22, ...), custom_call_target="tpu_custom_call" | custom-call | tf_op jit(solution)/shard_map/middle_block/pallas_call | solution.py:810
  56.6 0.7 %copy.20 = bf16[2,128,512]{2,1,0:T(8,128)(2,1)} copy(bf16[2,128,512]{2,1,0:T(8,128)(2,1)S(1)} %bitcast.14) | data formatting | bytes 524288

commit v5 on v4

--- a/solution.py
+++ b/solution.py
@@ -105,9 +105,8 @@
     return unfold(wide[:PARTS]), unfold(wide[PARTS:])
 
 
-def silu(values):
-    half = 0.5 * values
-    return half + half * jnp.tanh(half)
+def silu_of_double(values):
+    return values + values * jnp.tanh(values)
 
 
 def block_kernel(
@@ -248,9 +247,8 @@
         for sem in (s_send, s_recv):
             pltpu.make_async_copy(others, others, sem.at[phase]).wait()
         mean, inverse = merged_stats(stat_in[phase], n * WIDTH)
-        norm[0:1] = mean
-        norm[1:2] = inverse * gain[...]
-        norm[2:3] = shift[...]
+        norm[0:1] = inverse * gain[...]
+        norm[1:2] = shift[...] - mean * (inverse * gain[...])
 
     def put_stats(phase, values):
         packed = local_stats(values)
@@ -258,7 +256,7 @@
         stat_in[phase, 0] = packed
 
     def normalize(values):
-        return (values - norm[0:1]) * norm[1:2] + norm[2:3]
+        return values * norm[0:1] + norm[1:2]
 
     def halo_plan(phase, first_row, last_row):
         first, last = col_out.at[phase, 0], col_out.at[phase, 1]
@@ -314,32 +312,38 @@
         left, right = head > 0, head < heads - 1
         up, down = tile > 0, tile < tiles - 1
 
+        slope, level = 0.5 * norm[0:1], 0.5 * norm[1:2]
+
         def active(x):
-            return silu(normalize(x))
+            return silu_of_double(x * slope + level)
 
         for r in range(rows):
-            act[1 + r, PAD : PAD + cols] = active(values(r))
+            one = active(values(r))
+            act[1 + r, PAD : PAD + cols] = one
+            shifted[1, 1 + r] = one.astype(jnp.bfloat16)
             for side, at, inside in ((0, PAD - 1, left), (1, PAD + cols, right)):
                 one = active(col_in[phase, side, r])
                 act[1 + r, at : at + 1] = jnp.where(inside, one, 0.0)
         for side, at, inside in ((0, 0, up), (1, rows + 1, down)):
             one = active(row_in[phase, side].astype(jnp.float32))
-            act[at, PAD : PAD + cols] = jnp.where(inside, one, 0.0)
+            one = jnp.where(inside, one, 0.0)
+            act[at, PAD : PAD + cols] = one
+            shifted[1, at] = one.astype(jnp.bfloat16)
             for k, place, beside in ((0, PAD - 1, left), (1, PAD + cols, right)):
                 one = active(corner_in[phase, 2 * side + k])
                 both = jnp.logical_and(inside, beside)
                 act[at, place : place + 1] = jnp.where(both, one, 0.0)
-        for dj in range(3):
+        for dj in (0, 2):
             start = PAD - 1 + dj
             for r in range(rows + 2):
                 shifted[dj, r] = act[r, start : start + cols].astype(jnp.bfloat16)
 
-    def conv(weight):
+    def conv(weight, first=0, many=rows):
         result = None
         for di in range(3):
             for dj in range(3):
                 tap = 3 * di + dj
-                lhs = shifted[dj, di : di + rows].reshape(n, C)
+                lhs = shifted[dj, first + di : first + di + many].reshape(many * cols, C)
                 one = nn_dot(lhs, weight[tap * C : (tap + 1) * C])
                 result = one if result is None else result + one
         return result
@@ -384,13 +388,11 @@
         activate(1, lambda r: hid[r])
     with jax.named_scope("conv1"):
         weights[1].wait()
-        res[...] = (
-            lat_ref[...].astype(jnp.float32).reshape(n, C) + (conv(w2) + c2b[...])
-        ).astype(jnp.bfloat16)
-
-    with jax.named_scope("stats2"):
-        put_stats(2, res[...].astype(jnp.float32))
-        stats_start(2)
+
+    def residual(r):
+        with jax.named_scope("conv1"):
+            new = lat_ref[r].astype(jnp.float32) + (conv(w2, r, 1) + c2b[...])
+            res[r * cols : (r + 1) * cols] = new.astype(jnp.bfloat16)
 
     def piece(ref, ch):
         return ref.at[pl.ds(ch * (n // CHUNKS), n // CHUNKS)]
@@ -409,14 +411,22 @@
 
     at_end = jnp.logical_or(head == 0, head == heads - 1)
 
-    def straight(fn):
+    def straight(fn, opening=None):
         nearer = [(1, ch) for ch in range(CHUNKS)]
         farther = [(d, ch) for d in range(2, min(DIRECT, heads - 1) + 1) for ch in range(CHUNKS)]
         for chosen, order in ((at_end, interleaved(farther, nearer)), (~at_end, farther + nearer)):
             for distance, ch in order:
                 for way in (0, 1):
-
-                    @pl.when(jnp.logical_and(reachable(way, distance), chosen))
+                    present = jnp.logical_and(reachable(way, distance), chosen)
+                    if opening is not None:
+                        opens = ch == 0 and distance <= 2
+                        if opens and distance == 1:
+                            alone = ~reachable(way, 2)
+                            present = jnp.logical_and(present, alone if opening else ~alone)
+                        elif opens != opening:
+                            continue
+
+                    @pl.when(present)
                     def _(way=way, distance=distance, ch=ch):
                         fn(z_copy(head, res, way, distance, ch))
 
@@ -448,17 +458,28 @@
             partner,
         )
 
-    def q_copy(j):
+    def q_copy(j, part):
+        rows_of = pl.ds(0, n // 4) if part == 0 else pl.ds(n // 4, n - n // 4)
         return remote(
-            res, qn.at[j], q_send.at[j], q_recv.at[j], (fellow(j), head)
+            res.at[rows_of],
+            qn.at[j, rows_of],
+            q_send.at[j, part],
+            q_recv.at[j, part],
+            (fellow(j), head),
         )
 
-    def q_begin(j, carry):
-        q_copy(j).start()
-        return carry
-
+    residual(0)
+    straight(lambda copy: copy.start(), True)
+    for j in (1, 2):
+        if j < half:
+            q_copy(j, 0).start()
+    for r in range(1, rows):
+        residual(r)
     for ch in range(CHUNKS):
         c_copy(head, res, ch).start()
+    with jax.named_scope("stats2"):
+        put_stats(2, res[...].astype(jnp.float32))
+        stats_start(2)
 
     def pass_on(ch):
         def go(copy):
@@ -469,8 +490,17 @@
             for distance in range(DIRECT, heads - 1):
                 onward(distance, go, (ch,))
 
-    straight(lambda copy: copy.start())
-    lax.fori_loop(1, half, q_begin, 0)
+    straight(lambda copy: copy.start(), False)
+    for j in (1, 2):
+        if j < half:
+            q_copy(j, 1).start()
+
+    def q_begin(j, carry):
+        for part in range(2):
+            q_copy(j, part).start()
+        return carry
+
+    lax.fori_loop(3, half, q_begin, 0)
     pass_on(0)
     pass_on(1)
     with jax.named_scope("norm2"):
@@ -513,9 +543,9 @@
         fade = jnp.exp2(before - peak)
         sums, values = low[pair] * fade, None
         for one, (_, turned) in zip(scores, blocks):
-            expo = jnp.exp2(one - peak).astype(jnp.bfloat16)
-            sums = sums + jnp.sum(expo.astype(jnp.float32), axis=0, keepdims=True)
-            part = nn_dot(turned[...], expo)
+            expo = jnp.exp2(one - peak)
+            sums = sums + jnp.sum(expo, axis=0, keepdims=True)
+            part = nn_dot(turned[...], expo.astype(jnp.bfloat16))
             values = part if values is None else values + part
         top[pair] = peak
         low[pair] = sums
@@ -539,7 +569,8 @@
         make_query(0, 0, res[...])
         prepare(0, head, res[...])
     with jax.named_scope("q_wait0"):
-        q_copy(1).wait()
+        for part in range(2):
+            q_copy(1, part).wait()
     pass_on(2)
     with jax.named_scope("query1"):
         make_query(0, 1, qn[1])
@@ -580,16 +611,17 @@
         with jax.named_scope("together"):
             other_pairs(both_cores(source))
 
-    def own(source, distance, way):
+    def own_pair():
         with jax.named_scope("own_far"):
-            attend(0, both_cores(source))
+            attend(0, *[both_cores(lax.rem(head + k, heads)) for k in range(1, heads)])
 
     columns(begin, (1,), at_end)
 
     def rest(pair, carry):
         with jax.named_scope("q_wait1"):
             for at in range(2):
-                q_copy(2 * pair + at).wait()
+                for part in range(2):
+                    q_copy(2 * pair + at, part).wait()
         with jax.named_scope("query2"):
             clear(pair)
             for at in range(2):
@@ -604,22 +636,32 @@
     columns(together, (1,), at_end)
     columns(together, (2,))
 
-    def apart(*places):
-        sources = [source for source, _, _ in places]
-        for place in places:
-            begin(*place)
+    def apart(*place):
+        begin(*place)
         with jax.named_scope("late0"):
-            other_pairs(*[one_core(0, source) for source in sources])
-        for source in sources:
-            second(source)
+            other_pairs(one_core(0, place[0]))
+        second(place[0])
         with jax.named_scope("late1"):
-            other_pairs(*[one_core(1, source) for source in sources])
-
-    @pl.when(~at_end)
-    def _():
-        apart((head - 1, 1, 0), (head + 1, 1, 1))
-
-    columns(lambda *place: apart(place), far[1:])
+            other_pairs(one_core(1, place[0]))
+
+    def two_near(first, last):
+        begin(*first)
+        with jax.named_scope("late0"):
+            other_pairs(one_core(0, first[0]))
+        second(first[0])
+        begin(*last)
+        with jax.named_scope("late01"):
+            other_pairs(one_core(1, first[0]), one_core(0, last[0]))
+        second(last[0])
+        with jax.named_scope("late1"):
+            other_pairs(one_core(1, last[0]))
+
+    below, above = (head - 1, 1, 0), (head + 1, 1, 1)
+    lower = 2 * head < heads - 1
+    pl.when(jnp.logical_and(~at_end, lower))(lambda: two_near(below, above))
+    pl.when(jnp.logical_and(~at_end, ~lower))(lambda: two_near(above, below))
+
+    columns(apart, far[1:])
 
     def both(src, dst, src_level, dst_level, sem, device):
         return [
@@ -698,7 +740,7 @@
             begin_all(hop(1))
             finish(1, 0, o_out, l_out)
             begin_all(direct(2))
-        columns(own, tuple(range(1, heads)))
+        own_pair()
         with jax.named_scope("give1"):
             finish(0, 1, o_out, l_out)
             begin_all(direct(1))
@@ -728,7 +770,7 @@
             return carry
 
         lax.fori_loop(0, pairs - 1, give, 0)
-        columns(own, tuple(range(1, heads)))
+        own_pair()
         finish(0, 1, o_out, l_out)
         begin_all(give_copies(1))
         finish(0, 0, o_in, l_in)
@@ -857,8 +899,8 @@
             dma((heads, CHUNKS)),
             dma((heads, CHUNKS)),
             dma((heads, CHUNKS)),
-            dma((half,)),
-            dma((half,)),
+            dma((half, 2)),
+            dma((half, 2)),
             dma((half + 2,)),
             dma((half + 2,)),
             dma((half + 2,)),

time: 57.4 us -> 55.5 us (0.967)
  Pallas kernels: 56.6 us -> 54.6 us
    pallas_call x1, Pallas kernels: 56.6 us -> 54.6 us  [per_device(): pl.pallas_call(functools.partial(block_kernel, tiles, heads), out_shape=p...]
where the time goes in v5:
time: 55.5 us; the launch traced here: 55.3 us
  Pallas kernels  54.6 us (98%)
  local copies, waits for them, and re-layouts  0.71 us (1%)
    pallas_call x1, Pallas kernels, per_device(): pl.pallas_call(functools.partial(block_kernel, tiles, heads), out_shape=p...  54.6 us

profile of v5, /device:TPU:0, one launch (start us, length us, event | category | flops | bytes accessed | tf_op | source)
XLA Modules:
  0.0 55.3 jit_solution(14408345437465110819)
XLA Ops:
  0.0 54.6 %middle_block.1 = bf16[256,512]{1,0:T(8,128)(2,1)S(1)} custom-call(bf16[2,128,512]{2,1,0:T(8,128)(2,1)} %lat_hbm.1, f32[1,512]{1,0:T(1,128)} %bitcast.17, f32[1,512]{1,0:T(1,128)} %bitcast.18, f32[1,512]{1,0:T(1,128)} %bitcast.19, f32[1,512]{1,0:T(1,128)} %bitcast.20, f32[1,512]{1,0:T(1,128)} %bitcast.21, f32[1,512]{1,0:T(1,128)} %bitcast.22, ...), custom_call_target="tpu_custom_call" | custom-call | tf_op jit(solution)/shard_map/middle_block/pallas_call | solution.py:852
  54.6 0.7 %copy.20 = bf16[2,128,512]{2,1,0:T(8,128)(2,1)} copy(bf16[2,128,512]{2,1,0:T(8,128)(2,1)S(1)} %bitcast.14) | data formatting | bytes 524288

commit v6 on v5

--- a/solution.py
+++ b/solution.py
@@ -459,7 +459,7 @@
         )
 
     def q_copy(j, part):
-        rows_of = pl.ds(0, n // 4) if part == 0 else pl.ds(n // 4, n - n // 4)
+        rows_of = pl.ds(0, n // 2) if part == 0 else pl.ds(n // 2, n - n // 2)
         return remote(
             res.at[rows_of],
             qn.at[j, rows_of],

time: 55.5 us -> 55.3 us (level)
  no operation moved by 1% of the time
where the time goes in v6:
time: 55.3 us; the launch traced here: 55.1 us
  Pallas kernels  54.4 us (98%)
  local copies, waits for them, and re-layouts  0.71 us (1%)
    pallas_call x1, Pallas kernels, per_device(): pl.pallas_call(functools.partial(block_kernel, tiles, heads), out_shape=p...  54.4 us

profile of v6, /device:TPU:0, one launch (start us, length us, event | category | flops | bytes accessed | tf_op | source)
XLA Modules:
  0.0 55.1 jit_solution(8519200533443109944)
XLA Ops:
  0.0 54.4 %middle_block.1 = bf16[256,512]{1,0:T(8,128)(2,1)S(1)} custom-call(bf16[2,128,512]{2,1,0:T(8,128)(2,1)} %lat_hbm.1, f32[1,512]{1,0:T(1,128)} %bitcast.17, f32[1,512]{1,0:T(1,128)} %bitcast.18, f32[1,512]{1,0:T(1,128)} %bitcast.19, f32[1,512]{1,0:T(1,128)} %bitcast.20, f32[1,512]{1,0:T(1,128)} %bitcast.21, f32[1,512]{1,0:T(1,128)} %bitcast.22, ...), custom_call_target="tpu_custom_call" | custom-call | tf_op jit(solution)/shard_map/middle_block/pallas_call | solution.py:852
  54.4 0.7 %copy.20 = bf16[2,128,512]{2,1,0:T(8,128)(2,1)} copy(bf16[2,128,512]{2,1,0:T(8,128)(2,1)S(1)} %bitcast.14) | data formatting | bytes 524288

commit v7 on v6

--- a/solution.py
+++ b/solution.py
@@ -684,6 +684,11 @@
         for distance in range(DIRECT, heads - 1):
             onward(distance, lambda copy: copy.wait_send())
 
+    def fold_weights():
+        value_bias = jnp.broadcast_to(vb[...], (8, C)).astype(jnp.bfloat16)
+        norm[2:3] = nn_dot(value_bias, wp[3])[:1] + ob[...]
+        wp[0] = nn_dot(wp[2], wp[3]).astype(jnp.bfloat16)
+
     def begin_all(copies):
         for copy in copies:
             copy.start()
@@ -747,6 +752,7 @@
         with jax.named_scope("finish0"):
             finish(0, 0, o_in, l_in)
             column_sent()
+            fold_weights()
         with jax.named_scope("merge2"):
             merge(2)
         with jax.named_scope("merge1"):
@@ -775,6 +781,7 @@
         begin_all(give_copies(1))
         finish(0, 0, o_in, l_in)
         column_sent()
+        fold_weights()
         lax.fori_loop(1, half, take, 0)
         parts = half
     with jax.named_scope("last"):
@@ -793,8 +800,7 @@
             sides.append(side)
         mixed = jnp.concatenate(sides, axis=1)
         mixed = jnp.transpose(mixed.astype(jnp.bfloat16))
-        attended = (nn_dot(mixed, wp[2]) + vb[...]).astype(jnp.bfloat16)
-        out = nn_dot(attended, wp[3]) + ob[...]
+        out = nn_dot(mixed, wp[0]) + norm[2:3]
         out_ref[...] = (res[...].astype(jnp.float32) + out).astype(jnp.bfloat16)
 
 

time: 55.3 us -> 55.1 us (level)
  no operation moved by 1% of the time
where the time goes in v7:
time: 55.1 us; the launch traced here: 54.9 us
  Pallas kernels  54.2 us (98%)
  local copies, waits for them, and re-layouts  0.71 us (1%)
    pallas_call x1, Pallas kernels, per_device(): pl.pallas_call(functools.partial(block_kernel, tiles, heads), out_shape=p...  54.2 us

profile of v7, /device:TPU:0, one launch (start us, length us, event | category | flops | bytes accessed | tf_op | source)
XLA Modules:
  0.0 54.9 jit_solution(3901825172649268024)
XLA Ops:
  0.0 54.2 %middle_block.1 = bf16[256,512]{1,0:T(8,128)(2,1)S(1)} custom-call(bf16[2,128,512]{2,1,0:T(8,128)(2,1)} %lat_hbm.1, f32[1,512]{1,0:T(1,128)} %bitcast.17, f32[1,512]{1,0:T(1,128)} %bitcast.18, f32[1,512]{1,0:T(1,128)} %bitcast.19, f32[1,512]{1,0:T(1,128)} %bitcast.20, f32[1,512]{1,0:T(1,128)} %bitcast.21, f32[1,512]{1,0:T(1,128)} %bitcast.22, ...), custom_call_target="tpu_custom_call" | custom-call | tf_op jit(solution)/shard_map/middle_block/pallas_call | solution.py:858
  54.2 0.7 %copy.20 = bf16[2,128,512]{2,1,0:T(8,128)(2,1)} copy(bf16[2,128,512]{2,1,0:T(8,128)(2,1)S(1)} %bitcast.14) | data formatting | bytes 524288
